TPU v7x, 256 devices: a whole 4x4x8 slice. The times are simulated.
256 devices in a mesh: gz: 32 (over z, x_hi, core), vert: 8 (over y, x_lo).
Axes of the slice: x: 4 (x_hi: 2, x_lo: 2; x = x_hi * 2 + x_lo), y: 4, z: 8, core: 2. Of those that a mesh axis runs over, the one named last changes fastest.
Arguments:
- volume: float32 [256, 128, 1024], P('gz'), may hold values from -6 to 6
- angle_index: int32 [32], P('vert'), may hold values from 0 to 511
- detector_rows: int32 [128], replicated, may hold values from 0 to 127, each once
- measured: float32 [32, 128, 1024], P('vert', 'gz'), may hold values from -96 to 96
Outputs:
- residual: float32 [32, 128, 1024], P('vert', 'gz')
- gradient: float32 [256, 128, 1024], P('gz', 'vert')
All inputs are finite; a program needn't handle non-finite values.
Results may differ from a plain program's by a relative error of at most 0.0003.
Values sent between devices are 32-bit elements; how exact they have to be, the bound alone decides.
No kernel may reach another device: no remote copies, remote signals or barrier semaphores. Data moves between devices by JAX's collectives and lax.ppermute only.
A program may use at most 64 MiB of HBM per device.

v0:
```python
import jax
import jax.numpy as jnp
from jax import lax
from jax.sharding import PartitionSpec as P

ANGLES = 512


def in_blocks(value, dim, peers):
    dims = value.shape
    tiles = value.reshape(*dims[:dim], peers, dims[dim] // peers, *dims[dim + 1 :])
    return jnp.moveaxis(tiles, dim, 0)


def sent_and_summed(value, axis, dim):
    peers = lax.axis_size(axis)
    tiles = lax.all_to_all(in_blocks(value, dim, peers), axis, 0, 0, tiled=True)
    return jnp.sum(tiles, axis=0)


def in_order(tiles, dim):
    dims = list(tiles.shape[1:])
    dims[dim] *= tiles.shape[0]
    return jnp.moveaxis(tiles, 0, dim).reshape(dims)


def sent_to_all(value, axis):
    copies = jnp.broadcast_to(value, (lax.axis_size(axis), *value.shape))
    return lax.all_to_all(copies, axis, split_axis=0, concat_axis=0, tiled=True)


def gather_directly(value, axis, dim):
    return in_order(sent_to_all(value, axis), dim)


def shifts(depth_pos, angle_value):
    slope_num = 2 * angle_value - ANGLES
    product = depth_pos * slope_num
    shift_whole = jnp.floor_divide(product, ANGLES)
    shift_part = (product - shift_whole * ANGLES).astype(jnp.float32) / ANGLES
    slope_value = slope_num.astype(jnp.float32) / ANGLES
    weight = jnp.sqrt(1.0 + slope_value * slope_value)
    return (shift_whole, shift_part, weight)


def backproject(back, angles, depth_pos, margin):
    columns, row_count = (back.shape[2], back.shape[1])
    back_cols = jnp.transpose(back, (0, 2, 1))
    back_pad = jnp.pad(back_cols, ((0, 0), (margin, margin), (0, 0)))

    def add_view(running, view_item):
        plane, angle_value = view_item
        shift_whole, shift_part, weight = shifts(depth_pos, angle_value)

        def add_shifted(offset, fraction):
            window = lax.dynamic_slice_in_dim(plane, offset, columns + 1, 0)
            return (1.0 - fraction) * window[1:, :] + fraction * window[:-1, :]

        contrib = jax.vmap(add_shifted)(margin - shift_whole - 1, shift_part)
        return (running + weight * contrib, None)

    start_sum = jnp.zeros((depth_pos.shape[0], columns, row_count), jnp.float32)
    summed, _ = lax.scan(add_view, start_sum, (back_pad, angles))
    return jnp.transpose(summed, (0, 2, 1))


def per_device(volume, angle_index, detector_rows, measured):
    layers, row_count, columns = volume.shape
    slab_count = lax.axis_size("gz")
    total_depth = layers * slab_count
    margin = total_depth // 2 + 2
    depth_pos = (
        lax.axis_index("gz") * layers + jnp.arange(layers, dtype=jnp.int32) - total_depth // 2
    )
    vol_cols = jnp.transpose(volume, (0, 2, 1))
    padded = jnp.pad(vol_cols, ((0, 0), (margin, margin), (0, 0)))

    def project(angle_value):
        shift_whole, shift_part, weight = shifts(depth_pos, angle_value)

        def project_shifted(plane, offset, fraction):
            window = lax.dynamic_slice_in_dim(plane, offset, columns + 1, 0)
            return (1.0 - fraction) * window[:-1, :] + fraction * window[1:, :]

        contrib = jax.vmap(project_shifted)(padded, margin + shift_whole, shift_part)
        return weight * jnp.sum(contrib, axis=0)

    partial_cols = lax.map(project, angle_index)
    det_cols = jnp.take(partial_cols, detector_rows, axis=2)
    det_order = jnp.transpose(det_cols, (0, 2, 1))
    res_scale = total_depth ** (-0.5)
    own_rows = sent_and_summed(det_order, "gz", 1)
    residual = (own_rows - measured) * res_scale
    full_rows = gather_directly(residual, "gz", 1)
    back = jnp.zeros_like(full_rows).at[:, detector_rows, :].set(full_rows)
    view_scale = (angle_index.shape[0] * lax.axis_size("vert")) ** (-0.5)
    contrib_all = backproject(back, angle_index, depth_pos, margin)
    gradient = sent_and_summed(contrib_all, "vert", 1) * view_scale
    return (residual, gradient)


def solution(mesh):
    in_specs = (P("gz", None, None), P("vert"), P(), P("vert", "gz", None))
    out_specs = (P("vert", "gz", None), P("gz", "vert", None))
    return jax.shard_map(
        per_device, mesh=mesh, in_specs=in_specs, out_specs=out_specs, check_vma=False
    )
```

profile of v0, /device:TPU:4, one launch (start us, length us, event | category | flops | bytes accessed | tf_op | source)
XLA Modules:
  0.0 514.3 jit_solution(4433344700342288015)
XLA Ops:
  2.0 5.4 %copy.14 = f32[8,128,1024]{1,2,0:T(8,128)} copy(f32[8,128,1024]{2,1,0:T(8,128)} %param.8) | data formatting | bytes 8388608 | tf_op args[0]
  7.3 4.8 pad.20
  12.2 189.6 %while.36 = (s32[]{:T(128)}, f32[4,1024,128]{1,0,2:T(4,128)}, s32[4]{0:T(128)S(1)}, f32[8,1284,128]{2,1,0:T(8,128)}, s32[]{:T(128)}, /*index=5*/s32[]{:T(128)}, ...) while((s32[]{:T(128)}, f32[4,1024,128]{1,0,2:T(4,128)}, ...), condition=%wide.region_2.3_spmd.clone, body=%wide.region_0.2_spmd.clone.sunk | while | flops 4194698 | bytes 13117662 | solution.py:88
  13.4 30.7 %while.39 = (s32[]{:T(128)}, f32[8,1284,128]{2,1,0:T(8,128)}, s32[8,3]{0,1:T(4,128)S(1)}, f32[8,1025,128]{2,1,0:T(8,128)}, s32[]{:T(128)}) while((s32[]{:T(128)}, f32[8,1284,128]{2,1,0:T(8,128)}, s32[8,3]{0,1:T(4,128)S(1)}, f32[8,1025,128]{2,1,0:T(8,128)}, s32[]{:T(128)}) %tuple.117), condition=%wide.while_cond, body=%wide.while_body.sunk | while | flops 2 | bytes 1058409 | solution.py:82
  14.1 3.2 dynamic-slice_dynamic-update-slice_fusion.2
  17.9 3.2 dynamic-slice_dynamic-update-slice_fusion.2
  21.8 3.2 dynamic-slice_dynamic-update-slice_fusion.2
  25.6 3.2 dynamic-slice_dynamic-update-slice_fusion.2
  29.4 3.1 dynamic-slice_dynamic-update-slice_fusion.2
  33.3 3.2 dynamic-slice_dynamic-update-slice_fusion.2
  37.1 3.2 dynamic-slice_dynamic-update-slice_fusion.2
  41.0 3.2 dynamic-slice_dynamic-update-slice_fusion.2
  44.2 4.4 add_reduce_fusion.2
  49.1 10.5 %dynamic_update_slice.9 = f32[4,1024,128]{1,0,2:T(4,128)} dynamic-update-slice(f32[4,1024,128]{1,0,2:T(4,128)} %get-tuple-element.501, f32[1,1024,128]{1,0,2:T(1,128)S(1)} %copy.32, s32[]{:T(128)} %get-tuple-element.500, s32[]{:T(128)} %constant.248.clone.1..sunk, s32[]{:T(128)} %constant.248.clone.1..sunk) | dynamic-update-slice | bytes 1048580 | tf_op jit(solution)/shard_map/while/body/jit(dynamic_update_index_in_dim)/dynamic_update_slice | solution.py:88
  60.8 30.7 %while.39 = (s32[]{:T(128)}, f32[8,1284,128]{2,1,0:T(8,128)}, s32[8,3]{0,1:T(4,128)S(1)}, f32[8,1025,128]{2,1,0:T(8,128)}, s32[]{:T(128)}) while((s32[]{:T(128)}, f32[8,1284,128]{2,1,0:T(8,128)}, s32[8,3]{0,1:T(4,128)S(1)}, f32[8,1025,128]{2,1,0:T(8,128)}, s32[]{:T(128)}) %tuple.117), condition=%wide.while_cond, body=%wide.while_body.sunk | while | flops 2 | bytes 1058409 | solution.py:82
  61.5 3.2 dynamic-slice_dynamic-update-slice_fusion.2
  65.3 3.2 dynamic-slice_dynamic-update-slice_fusion.2
  69.2 3.2 dynamic-slice_dynamic-update-slice_fusion.2
  73.0 3.2 dynamic-slice_dynamic-update-slice_fusion.2
  76.9 3.1 dynamic-slice_dynamic-update-slice_fusion.2
  80.7 3.2 dynamic-slice_dynamic-update-slice_fusion.2
  84.5 3.2 dynamic-slice_dynamic-update-slice_fusion.2
  88.4 3.2 dynamic-slice_dynamic-update-slice_fusion.2
  91.6 4.4 add_reduce_fusion.2
  96.5 10.5 %dynamic_update_slice.9 = f32[4,1024,128]{1,0,2:T(4,128)} dynamic-update-slice(f32[4,1024,128]{1,0,2:T(4,128)} %get-tuple-element.501, f32[1,1024,128]{1,0,2:T(1,128)S(1)} %copy.32, s32[]{:T(128)} %get-tuple-element.500, s32[]{:T(128)} %constant.248.clone.1..sunk, s32[]{:T(128)} %constant.248.clone.1..sunk) | dynamic-update-slice | bytes 1048580 | tf_op jit(solution)/shard_map/while/body/jit(dynamic_update_index_in_dim)/dynamic_update_slice | solution.py:88
  108.2 30.7 %while.39 = (s32[]{:T(128)}, f32[8,1284,128]{2,1,0:T(8,128)}, s32[8,3]{0,1:T(4,128)S(1)}, f32[8,1025,128]{2,1,0:T(8,128)}, s32[]{:T(128)}) while((s32[]{:T(128)}, f32[8,1284,128]{2,1,0:T(8,128)}, s32[8,3]{0,1:T(4,128)S(1)}, f32[8,1025,128]{2,1,0:T(8,128)}, s32[]{:T(128)}) %tuple.117), condition=%wide.while_cond, body=%wide.while_body.sunk | while | flops 2 | bytes 1058409 | solution.py:82
  108.9 3.2 dynamic-slice_dynamic-update-slice_fusion.2
  112.8 3.2 dynamic-slice_dynamic-update-slice_fusion.2
  116.6 3.2 dynamic-slice_dynamic-update-slice_fusion.2
  120.4 3.2 dynamic-slice_dynamic-update-slice_fusion.2
  124.3 3.1 dynamic-slice_dynamic-update-slice_fusion.2
  128.1 3.2 dynamic-slice_dynamic-update-slice_fusion.2
  131.9 3.2 dynamic-slice_dynamic-update-slice_fusion.2
  135.8 3.2 dynamic-slice_dynamic-update-slice_fusion.2
  139.0 4.4 add_reduce_fusion.2
  143.9 10.5 %dynamic_update_slice.9 = f32[4,1024,128]{1,0,2:T(4,128)} dynamic-update-slice(f32[4,1024,128]{1,0,2:T(4,128)} %get-tuple-element.501, f32[1,1024,128]{1,0,2:T(1,128)S(1)} %copy.32, s32[]{:T(128)} %get-tuple-element.500, s32[]{:T(128)} %constant.248.clone.1..sunk, s32[]{:T(128)} %constant.248.clone.1..sunk) | dynamic-update-slice | bytes 1048580 | tf_op jit(solution)/shard_map/while/body/jit(dynamic_update_index_in_dim)/dynamic_update_slice | solution.py:88
  155.6 30.7 %while.39 = (s32[]{:T(128)}, f32[8,1284,128]{2,1,0:T(8,128)}, s32[8,3]{0,1:T(4,128)S(1)}, f32[8,1025,128]{2,1,0:T(8,128)}, s32[]{:T(128)}) while((s32[]{:T(128)}, f32[8,1284,128]{2,1,0:T(8,128)}, s32[8,3]{0,1:T(4,128)S(1)}, f32[8,1025,128]{2,1,0:T(8,128)}, s32[]{:T(128)}) %tuple.117), condition=%wide.while_cond, body=%wide.while_body.sunk | while | flops 2 | bytes 1058409 | solution.py:82
  156.3 3.2 dynamic-slice_dynamic-update-slice_fusion.2
  160.2 3.2 dynamic-slice_dynamic-update-slice_fusion.2
  164.0 3.2 dynamic-slice_dynamic-update-slice_fusion.2
  167.8 3.2 dynamic-slice_dynamic-update-slice_fusion.2
  175.5 3.2 dynamic-slice_dynamic-update-slice_fusion.2
  179.3 3.2 dynamic-slice_dynamic-update-slice_fusion.2
  183.2 3.2 dynamic-slice_dynamic-update-slice_fusion.2
  186.4 4.4 add_reduce_fusion.2
  191.3 10.5 %dynamic_update_slice.9 = f32[4,1024,128]{1,0,2:T(4,128)} dynamic-update-slice(f32[4,1024,128]{1,0,2:T(4,128)} %get-tuple-element.501, f32[1,1024,128]{1,0,2:T(1,128)S(1)} %copy.32, s32[]{:T(128)} %get-tuple-element.500, s32[]{:T(128)} %constant.248.clone.1..sunk, s32[]{:T(128)} %constant.248.clone.1..sunk) | dynamic-update-slice | bytes 1048580 | tf_op jit(solution)/shard_map/while/body/jit(dynamic_update_index_in_dim)/dynamic_update_slice | solution.py:88
  201.8 3.4 gather_fusion
  205.8 62.9 %all_to_all.15 = f32[32,4,4,1024]{3,1,2,0:T(4,128)S(1)} all-to-all(f32[32,4,4,1024]{3,1,2,0:T(4,128)S(1)} %bitcast.72), channel_id=1, replica_groups=mesh['gz'=32,'vert'=8] {'gz'}, dimensions={0} | all-to-all | bytes 4194304 | tf_op jit(solution)/shard_map/all_to_all | solution.py:17
  271.1 5.0 all-to-all-start.1
  276.1 50.2 %all-to-all-done.1 = f32[32,4,4,1024]{3,1,2,0:T(4,128)S(1)} async-done(((f32[32,4,4,1024]{3,1,2,0:T(4,128)}), f32[32,4,4,1024]{3,1,2,0:T(4,128)S(1)}, u32[]{:S(2)}, u32[]{:S(2)}) %all-to-all-start.1) | async-done | bytes 2097184 | tf_op jit(solution)/shard_map/all_to_all | solution.py:29
  328.1 11.8 %scatter_fusion = f32[4,128,1024]{2,0,1:T(4,128)S(1)} fusion(f32[4,128,1024]{2,0,1:T(4,128)S(1)} %broadcast_in_dim.38, s32[128]{0:T(128)S(1)} %compare_select_fusion.14, f32[128,4,1024]{2,1,0:T(4,128)} %bitcast.71), kind=kCustom, calls=%fused_computation.1 | custom fusion | bytes 6291968 | tf_op jit(solution)/shard_map/scatter | solution.py:95
  343.6 102.3 %while.38 = (s32[]{:T(128)}, f32[8,1024,128]{2,1,0:T(8,128)}, s32[4]{0:T(128)S(1)}, f32[4,1284,128]{2,1,0:T(8,128)S(1)}, s32[]{:T(128)}, /*index=5*/s32[]{:T(128...) while((s32[]{:T(128)}, f32[8,1024,128]{2,1,0:T(8,128)}, ...), condition=%wide.region_6.7_spmd.clone, body=%wide.region_5.6_spmd.clone.sunk | while | flops 6291827 | bytes 19146876 | solution.py:63
  344.9 16.7 %while.40 = (s32[]{:T(128)}, f32[1284,128]{1,0:T(8,128)S(1)}, s32[8,2]{0,1:T(2,128)S(1)}, f32[8,1025,128]{2,1,0:T(8,128)}, s32[]{:T(128)}) while((s32[]{:T(128)}, f32[1284,128]{1,0:T(8,128)S(1)}, s32[8,2]{0,1:T(2,128)S(1)}, f32[8,1025,128]{2,1,0:T(8,128)}, s32[]{:T(128)}) %tuple.114), condition=%wide.while_cond.1, body=%wide.while_body.1.sunk | while | flops 2 | bytes 1054297 | solution.py:56
  361.7 6.6 %select_add_fusion.2 = f32[8,1024,128]{2,1,0:T(8,128)} fusion(f32[8,1024,128]{2,1,0:T(8,128)} %get-tuple-element.537, f32[8,1025,128]{2,1,0:T(8,128)} %get-tuple-element.444, f32[8]{0:T(128)S(1)} %get-tuple-element.445, f32[8]{0:T(128)S(1)} %get-tuple-element.446, f32[]{:T(128)S(6)} %sqrt.21, pred[]{:T(512)S(6)} %compare.81), kind=kLoop, calls=%fused_computation.24.clone.1 | loop fusion | flops 6291456 | bytes 16777284 | tf_op jit(solution)/shard_map/while/body/eval_jaxpr/add | solution.py:60
  369.6 16.7 %while.40 = (s32[]{:T(128)}, f32[1284,128]{1,0:T(8,128)S(1)}, s32[8,2]{0,1:T(2,128)S(1)}, f32[8,1025,128]{2,1,0:T(8,128)}, s32[]{:T(128)}) while((s32[]{:T(128)}, f32[1284,128]{1,0:T(8,128)S(1)}, s32[8,2]{0,1:T(2,128)S(1)}, f32[8,1025,128]{2,1,0:T(8,128)}, s32[]{:T(128)}) %tuple.114), condition=%wide.while_cond.1, body=%wide.while_body.1.sunk | while | flops 2 | bytes 1054297 | solution.py:56
  386.4 7.8 %select_add_fusion.2 = f32[8,1024,128]{2,1,0:T(8,128)} fusion(f32[8,1024,128]{2,1,0:T(8,128)} %get-tuple-element.537, f32[8,1025,128]{2,1,0:T(8,128)} %get-tuple-element.444, f32[8]{0:T(128)S(1)} %get-tuple-element.445, f32[8]{0:T(128)S(1)} %get-tuple-element.446, f32[]{:T(128)S(6)} %sqrt.21, pred[]{:T(512)S(6)} %compare.81), kind=kLoop, calls=%fused_computation.24.clone.1 | loop fusion | flops 6291456 | bytes 16777284 | tf_op jit(solution)/shard_map/while/body/eval_jaxpr/add | solution.py:60
  395.5 16.7 %while.40 = (s32[]{:T(128)}, f32[1284,128]{1,0:T(8,128)S(1)}, s32[8,2]{0,1:T(2,128)S(1)}, f32[8,1025,128]{2,1,0:T(8,128)}, s32[]{:T(128)}) while((s32[]{:T(128)}, f32[1284,128]{1,0:T(8,128)S(1)}, s32[8,2]{0,1:T(2,128)S(1)}, f32[8,1025,128]{2,1,0:T(8,128)}, s32[]{:T(128)}) %tuple.114), condition=%wide.while_cond.1, body=%wide.while_body.1.sunk | while | flops 2 | bytes 1054297 | solution.py:56
  412.3 7.8 %select_add_fusion.2 = f32[8,1024,128]{2,1,0:T(8,128)} fusion(f32[8,1024,128]{2,1,0:T(8,128)} %get-tuple-element.537, f32[8,1025,128]{2,1,0:T(8,128)} %get-tuple-element.444, f32[8]{0:T(128)S(1)} %get-tuple-element.445, f32[8]{0:T(128)S(1)} %get-tuple-element.446, f32[]{:T(128)S(6)} %sqrt.21, pred[]{:T(512)S(6)} %compare.81), kind=kLoop, calls=%fused_computation.24.clone.1 | loop fusion | flops 6291456 | bytes 16777284 | tf_op jit(solution)/shard_map/while/body/eval_jaxpr/add | solution.py:60
  421.4 16.7 %while.40 = (s32[]{:T(128)}, f32[1284,128]{1,0:T(8,128)S(1)}, s32[8,2]{0,1:T(2,128)S(1)}, f32[8,1025,128]{2,1,0:T(8,128)}, s32[]{:T(128)}) while((s32[]{:T(128)}, f32[1284,128]{1,0:T(8,128)S(1)}, s32[8,2]{0,1:T(2,128)S(1)}, f32[8,1025,128]{2,1,0:T(8,128)}, s32[]{:T(128)}) %tuple.114), condition=%wide.while_cond.1, body=%wide.while_body.1.sunk | while | flops 2 | bytes 1054297 | solution.py:56
  438.1 7.8 %select_add_fusion.2 = f32[8,1024,128]{2,1,0:T(8,128)} fusion(f32[8,1024,128]{2,1,0:T(8,128)} %get-tuple-element.537, f32[8,1025,128]{2,1,0:T(8,128)} %get-tuple-element.444, f32[8]{0:T(128)S(1)} %get-tuple-element.445, f32[8]{0:T(128)S(1)} %get-tuple-element.446, f32[]{:T(128)S(6)} %sqrt.21, pred[]{:T(512)S(6)} %compare.81), kind=kLoop, calls=%fused_computation.24.clone.1 | loop fusion | flops 6291456 | bytes 16777284 | tf_op jit(solution)/shard_map/while/body/eval_jaxpr/add | solution.py:60
  445.9 5.4 %copy.18 = f32[8,1024,128]{1,2,0:T(8,128)} copy(f32[8,1024,128]{2,1,0:T(8,128)} %get-tuple-element.200) | data formatting | bytes 8388608 | tf_op jit(solution)/shard_map/while | solution.py:63
  451.3 4.7 copy.19
  456.0 5.1 all-to-all-start.2
  461.8 49.1 %all-to-all-done.2 = f32[8,8,16,1024]{3,2,1,0:T(8,128)} async-done(((f32[8,8,16,1024]{3,2,1,0:T(8,128)}), f32[8,8,16,1024]{3,2,1,0:T(8,128)}, u32[]{:S(2)}, u32[]{:S(2)}) %all-to-all-start.2) | async-done | bytes 4194336 | tf_op jit(solution)/shard_map/all_to_all | solution.py:17
  (238 shorter events, 112.4 us)
Async XLA Ops:
  7.3 4.8 copy-start.2
  205.8 63.4 %copy-start.1 = (f32[4,4,1024]{2,1,0:T(4,128)S(1)}, f32[4,4,1024]{2,1,0:T(4,128)}, u32[]{:S(2)}) copy-start(f32[4,4,1024]{2,1,0:T(4,128)} %param.11) | copy-start | bytes 196612
  271.1 55.2 %all-to-all-start.1 = ((f32[32,4,4,1024]{3,1,2,0:T(4,128)}), f32[32,4,4,1024]{3,1,2,0:T(4,128)S(1)}, u32[]{:S(2)}, u32[]{:S(2)}) async-start(f32[32,4,4,1024]{3,1,2,0:T(4,128)} %broadcast_in_dim.39), calls=%async_computation.1 | async-start | bytes 4194304 | tf_op jit(solution)/shard_map/all_to_all | solution.py:29
  326.2 1.3 copy-start
  456.0 54.9 %all-to-all-start.2 = ((f32[8,8,16,1024]{3,2,1,0:T(8,128)}), f32[8,8,16,1024]{3,2,1,0:T(8,128)}, u32[]{:S(2)}, u32[]{:S(2)}) async-start(f32[8,8,16,1024]{3,2,1,0:T(8,128)} %copy.19), calls=%async_computation.2 | async-start | bytes 8388608 | tf_op jit(solution)/shard_map/all_to_all | solution.py:17
where the time goes:
time: 519 us; the launch traced here: 514 us
  local copies, waits for them, and re-layouts  282 us (54%)
  waiting for transfers between devices  99.3 us (19%)
  blocking collectives  62.9 us (12%)
  other arithmetic  53.8 us (10%)
  starting transfers between devices  10.1 us (2%)
  loops' own time  5.7 us (1%)
    gather x192, local copies, waits for them, and re-layouts  190 us
    all_to_all x1, blocking collectives, sent_and_summed(): tiles = lax.all_to_all(in_blocks(value, dim, peers), axis, 0, 0, tiled=True)  62.9 us
    all_to_all x1, waiting for transfers between devices, sent_to_all(): return lax.all_to_all(copies, axis, split_axis=0, concat_axis=0, tiled=True)  50.2 us
    all_to_all x1, waiting for transfers between devices, sent_and_summed(): tiles = lax.all_to_all(in_blocks(value, dim, peers), axis, 0, 0, tiled=True)  49.1 us
    dynamic_update_slice x8, local copies, waits for them, and re-layouts, per_device(): partial_cols = lax.map(project, angle_index)  43.7 us
    add x4, other arithmetic, add_view(): return (running + weight * contrib, None)  29.9 us
    reduce_sum x4, other arithmetic, project(): return weight * jnp.sum(contrib, axis=0)  17.6 us
    scatter x1, local copies, waits for them, and re-layouts, per_device(): back = jnp.zeros_like(full_rows).at[:, detector_rows, :].set(full_rows)  11.8 us
  transfers between devices with their start and end apart: 2, of which 2 were waited for; matrix products, arithmetic and copies ran while one was open for 0% of the time, Pallas kernels for 0%

commit v1 on v0

v1 whole, which is shorter than its diff:
```python
import functools

import jax
import jax.numpy as jnp
from jax import lax
from jax.experimental import pallas as pl
from jax.experimental.pallas import tpu as pltpu
from jax.sharding import PartitionSpec as P

ANGLES = 512
LANES = 128
VMEM = pltpu.VMEM
SMEM = pltpu.SMEM


def take_rows_kernel(rows_ref, half_ref, slab_ref, out_ref):
    peers = out_ref.shape[0]
    chunks = out_ref.shape[2]
    place = lax.broadcasted_iota(jnp.int32, (chunks, LANES), 0)

    def one(peer, carry):
        row = rows_ref[peer]
        start = pl.multiple_of(row // 8 * 8, 8)
        inside = row - start
        found = None
        for chunk in range(chunks):
            tile = slab_ref[0, pl.ds(start, 8), pl.ds(chunk * LANES, LANES)]
            turned = pltpu.roll(tile, (chunk + 8 - inside) % 8, 0)
            found = turned if found is None else jnp.where(place == chunk, turned, found)
        out_ref[peer, 0] = found
        return carry

    lax.fori_loop(0, peers, one, 0, unroll=4)


def take_rows(volume, rows, half):
    layers, row_count, columns = volume.shape
    peers = rows.shape[0]
    part = layers // 2
    chunks = columns // LANES
    return pl.pallas_call(
        take_rows_kernel,
        grid_spec=pltpu.PrefetchScalarGridSpec(
            num_scalar_prefetch=2,
            grid=(part,),
            in_specs=[
                pl.BlockSpec(
                    (1, row_count, columns),
                    lambda layer, rows_ref, half_ref: (half_ref[0] * part + layer, 0, 0),
                )
            ],
            out_specs=pl.BlockSpec(
                (peers, 1, chunks, LANES), lambda layer, rows_ref, half_ref: (0, layer, 0, 0)
            ),
        ),
        out_shape=jax.ShapeDtypeStruct((peers, part, chunks, LANES), jnp.float32),
        name="take_rows",
    )(rows, half, volume)


def fill_padded(plain_ref, index, base_ref, diff_ref, ahead, scale=None):
    chunks = plain_ref.shape[1]
    rows = base_ref.shape[1]
    value = plain_ref[index]
    if scale is not None:
        value = value * scale
    base_ref[index, pl.ds(0, 8), :] = jnp.zeros((8, LANES), jnp.float32)
    base_ref[index, pl.ds(8, 8), :] = jnp.zeros((8, LANES), jnp.float32)
    base_ref[index, pl.ds(1, chunks), :] = value
    padded = base_ref[index]
    lane = lax.broadcasted_iota(jnp.int32, (rows, LANES), 1)
    if ahead:
        turned = pltpu.roll(padded, LANES - 1, 1)
        carried = pltpu.roll(turned, rows - 1, 0)
        near = jnp.where(lane == LANES - 1, carried, turned)
    else:
        turned = pltpu.roll(padded, 1, 1)
        carried = pltpu.roll(turned, 1, 0)
        near = jnp.where(lane == 0, carried, turned)
    diff_ref[index] = near - padded


def shifted(base_ref, diff_ref, index, first, turn, lane_from, fraction):
    low = base_ref[index, pl.ds(first, 8), :]
    high = base_ref[index, pl.ds(first + 1, 8), :]
    low_diff = diff_ref[index, pl.ds(first, 8), :]
    high_diff = diff_ref[index, pl.ds(first + 1, 8), :]
    value = jnp.where(lane_from, low, high)
    diff = jnp.where(lane_from, low_diff, high_diff)
    return pltpu.roll(value + fraction * diff, turn, 1)


def split(offset):
    negative = (offset < 0).astype(jnp.int32)
    count = offset + LANES * negative
    return 1 - negative, count, jnp.where(count == 0, 0, LANES - count)


def project_kernel(angles_ref, first_ref, planes_ref, out_ref, base_ref, diff_ref):
    views = out_ref.shape[0]
    total = planes_ref.shape[0]
    lane = lax.broadcasted_iota(jnp.int32, (8, LANES), 1)

    def fill(layer, carry):
        fill_padded(planes_ref, layer, base_ref, diff_ref, True)
        return carry

    lax.fori_loop(0, total, fill, 0, unroll=4)

    group = 16

    def one_view(view, carry):
        slope = 2 * angles_ref[view] - ANGLES

        def layers(step, sums):
            sums = list(sums)
            for item in range(group):
                layer = step * group + item
                depth = first_ref[0] + 8 * (layer // 4) + item % 4
                product = depth * slope
                whole = lax.shift_right_arithmetic(product, 9)
                part = (product - whole * ANGLES).astype(jnp.float32) * (1.0 / ANGLES)
                first, count, turn = split(whole)
                sums[item % 4] = sums[item % 4] + shifted(
                    base_ref, diff_ref, layer, first, turn, lane >= count, part
                )
            return tuple(sums)

        zero = jnp.zeros((8, LANES), jnp.float32)
        sums = lax.fori_loop(0, total // group, layers, (zero,) * 4)
        ratio = jnp.full((8, LANES), slope, jnp.int32).astype(jnp.float32) / ANGLES
        weight = jnp.sqrt(1.0 + ratio * ratio)
        out_ref[view] = weight * ((sums[0] + sums[1]) + (sums[2] + sums[3]))
        return carry

    lax.fori_loop(0, views, one_view, 0)


def project(planes, angles, first_depth):
    total, chunks, _ = planes.shape
    views = angles.shape[0]
    return pl.pallas_call(
        project_kernel,
        in_specs=[
            pl.BlockSpec(memory_space=SMEM),
            pl.BlockSpec(memory_space=SMEM),
            pl.BlockSpec(memory_space=VMEM),
        ],
        out_specs=pl.BlockSpec(memory_space=VMEM),
        out_shape=jax.ShapeDtypeStruct((views, chunks, LANES), jnp.float32),
        scratch_shapes=[VMEM((total, 16, LANES), jnp.float32)] * 2,
        name="project",
    )(angles, first_depth, planes)


def backproject_kernel(
    scale, angles_ref, first_ref, rows_ref, out_ref, base_ref, diff_ref
):
    slabs, height = out_ref.shape[0], out_ref.shape[1]
    views = angles_ref.shape[0]
    lane = lax.broadcasted_iota(jnp.int32, (8, LANES), 1)

    def fill(view, carry):
        slope = 2 * angles_ref[view] - ANGLES
        ratio = jnp.full((8, LANES), slope, jnp.int32).astype(jnp.float32) / ANGLES
        weight = jnp.sqrt(1.0 + ratio * ratio) * scale
        for row in range(height):
            fill_padded(rows_ref, view * height + row, base_ref, diff_ref, False, weight)
        return carry

    lax.fori_loop(0, views, fill, 0)

    group = 4

    def one_slab(slab, carry):
        depth = first_ref[0] + 8 * slab

        def some_views(step, sums):
            sums = list(sums)
            for item in range(group):
                view = step * group + item
                product = depth * (2 * angles_ref[view] - ANGLES)
                whole = lax.shift_right_arithmetic(product, 9)
                part = (product - whole * ANGLES).astype(jnp.float32) * (1.0 / ANGLES)
                first, count, turn = split(-whole)
                for row in range(height):
                    sums[row] = sums[row] + shifted(
                        base_ref, diff_ref, view * height + row, first, turn, lane >= count, part
                    )
            return tuple(sums)

        zero = jnp.zeros((8, LANES), jnp.float32)
        sums = lax.fori_loop(0, views // group, some_views, (zero,) * height)
        for row in range(height):
            out_ref[slab, row] = sums[row]
        return carry

    lax.fori_loop(0, slabs, one_slab, 0)


def backproject(rows, angles, first_depth, slabs, scale):
    views, height, chunks, _ = rows.shape
    return pl.pallas_call(
        functools.partial(backproject_kernel, scale),
        in_specs=[
            pl.BlockSpec(memory_space=SMEM),
            pl.BlockSpec(memory_space=SMEM),
            pl.BlockSpec(memory_space=VMEM),
        ],
        out_specs=pl.BlockSpec(memory_space=VMEM),
        out_shape=jax.ShapeDtypeStruct((slabs, height, chunks, LANES), jnp.float32),
        scratch_shapes=[VMEM((views * height, 16, LANES), jnp.float32)] * 2,
        name="backproject",
    )(angles, first_depth, rows.reshape(views * height, chunks, LANES))


def place_kernel(rows_ref, value_ref, out_ref):
    count = value_ref.shape[0]

    def one(row, carry):
        out_ref[rows_ref[row]] = value_ref[row]
        return carry

    lax.fori_loop(0, count, one, 0, unroll=8)


def place(value, rows):
    return pl.pallas_call(
        place_kernel,
        in_specs=[pl.BlockSpec(memory_space=SMEM), pl.BlockSpec(memory_space=VMEM)],
        out_specs=pl.BlockSpec(memory_space=VMEM),
        out_shape=jax.ShapeDtypeStruct(value.shape, jnp.float32),
        name="place",
    )(rows, value)


def swap(value, axis):
    return lax.all_to_all(value, axis, 0, 0, tiled=True)


def to_all(value, axis):
    return swap(jnp.broadcast_to(value, (lax.axis_size(axis), *value.shape)), axis)


def per_device(volume, angle_index, detector_rows, measured):
    layers, row_count, columns = volume.shape
    slabs = lax.axis_size("gz")
    groups = lax.axis_size("vert")
    own_views, height, _ = measured.shape
    chunks = columns // LANES
    depth = layers * slabs
    views = own_views * groups
    vert = lax.axis_index("vert")
    own_row, half = vert // 2, vert % 2
    angles = to_all(angle_index, "vert").reshape(views)

    wanted = lax.dynamic_index_in_dim(
        detector_rows.reshape(slabs, height), own_row, 1, keepdims=False
    )
    sent = take_rows(volume, wanted, half.reshape(1))
    planes = swap(sent, "gz").reshape(slabs * layers // 2, chunks, LANES)
    first = (half * (layers // 2) - depth // 2).reshape(1)
    partial = project(planes, angles, first)
    parts = swap(partial.reshape(groups, own_views, chunks, LANES), "vert")
    parts = parts.reshape(height, 2, own_views, chunks, LANES)
    summed = jnp.transpose(parts[:, 0] + parts[:, 1], (1, 0, 2, 3))
    rays = measured.reshape(own_views, height, chunks, LANES)
    own = (summed - rays) * depth ** (-0.5)
    residual = own.reshape(own_views, height, columns)

    full = to_all(own, "vert").reshape(views, height, chunks, LANES)
    first_back = (vert - depth // 2).reshape(1)
    contrib = backproject(full, angles, first_back, slabs, views ** (-0.5))
    layer = swap(contrib, "gz").reshape(row_count, chunks, LANES)
    ordered = place(layer, detector_rows)
    block = swap(ordered.reshape(groups, row_count // groups, chunks, LANES), "vert")
    gradient = block.reshape(layers, row_count // groups, columns)
    return (residual, gradient)


def solution(mesh):
    in_specs = (P("gz", None, None), P("vert"), P(), P("vert", "gz", None))
    out_specs = (P("vert", "gz", None), P("gz", "vert", None))
    return jax.shard_map(
        per_device, mesh=mesh, in_specs=in_specs, out_specs=out_specs, check_vma=False
    )
```

time: 519 us -> 206 us (0.40)
  local copies, waits for them, and re-layouts: 282 us -> 7.89 us
  Pallas kernels: 0 us -> 104 us
  waiting for transfers between devices: 99.3 us -> 40.2 us
  other arithmetic: 53.8 us -> 0.68 us
  blocking collectives: 62.9 us -> 22.9 us
  starting transfers between devices: 10.1 us -> 29.4 us
  loops' own time: 5.7 us -> 0 us
    gather x193 -> x0, local copies, waits for them, and re-layouts: 193 us -> none
    pallas_call x0 -> x4, Pallas kernels: none -> 104 us  [the longest x1 64.6 us: project(): pl.pallas_call(project_kernel, in_specs=[pl.BlockSpec(memory_space=SMEM),...]
    all_to_all x2 -> x5, waiting for transfers between devices: 99.3 us -> 40.2 us  [swap(): return lax.all_to_all(value, axis, 0, 0, tiled=True)]
    dynamic_update_slice x8 -> x0, local copies, waits for them, and re-layouts: 43.7 us -> none  [per_device(): partial_cols = lax.map(project, angle_index)]
    all_to_all x1, blocking collectives: 62.9 us -> 22.9 us  [swap(): return lax.all_to_all(value, axis, 0, 0, tiled=True)]
    add x4 -> x0, other arithmetic: 29.9 us -> none  [add_view(): return (running + weight * contrib, None)]
    reduce_sum x6 -> x0, other arithmetic: 20.7 us -> none  [the longest x4 17.6 us: project(): return weight * jnp.sum(contrib, axis=0)]
    all_to_all x2 -> x5, starting transfers between devices: 10.1 us -> 29.4 us  [swap(): return lax.all_to_all(value, axis, 0, 0, tiled=True)]
  transfers between devices with their start and end apart: 2 -> 5, of which waited for: 2 -> 4; matrix products, arithmetic and copies ran while one was open for 0% -> 2% of each run, Pallas kernels for 0% -> 3%
where the time goes in v1:
time: 206 us; the launch traced here: 205 us
  Pallas kernels  104 us (50%)
  waiting for transfers between devices  40.2 us (20%)
  starting transfers between devices  29.4 us (14%)
  blocking collectives  22.9 us (11%)
  local copies, waits for them, and re-layouts  7.89 us (4%)
    pallas_call x1, Pallas kernels, project(): pl.pallas_call(project_kernel, in_specs=[pl.BlockSpec(memory_space=SMEM),...  64.6 us
    all_to_all x5, waiting for transfers between devices, swap(): return lax.all_to_all(value, axis, 0, 0, tiled=True)  40.2 us
    pallas_call x1, Pallas kernels, backproject(): pl.pallas_call(functools.partial(backproject_kernel, scale), in_specs=[pl...  30.3 us
    all_to_all x5, starting transfers between devices, swap(): return lax.all_to_all(value, axis, 0, 0, tiled=True)  29.4 us
    all_to_all x1, blocking collectives, swap(): return lax.all_to_all(value, axis, 0, 0, tiled=True)  22.9 us
    pallas_call x1, Pallas kernels, take_rows(): pl.pallas_call(take_rows_kernel, grid_spec=pltpu.PrefetchScalarGridSpec(n...  6.66 us
  transfers between devices with their start and end apart: 5, of which 4 were waited for; matrix products, arithmetic and copies ran while one was open for 2% of the time, Pallas kernels for 3%

profile of v1, /device:TPU:4, one launch (start us, length us, event | category | flops | bytes accessed | tf_op | source)
XLA Modules:
  0.0 205.4 jit_solution(13563073085375551882)
XLA Ops:
  0.6 0.0 copy-start.2
  0.6 1.3 broadcast_in_dim.6
  1.9 5.1 %all-to-all-start = ((s32[8,1,4]{2,1,0:T(1,128)}), s32[8,1,4]{2,1,0:T(1,128)S(1)}, u32[]{:S(2)}, u32[]{:S(2)}) async-start(s32[8,1,4]{2,1,0:T(1,128)} %broadcast_in_dim.6), calls=%async_computation | async-start | bytes 8192 | tf_op jit(solution)/shard_map/all_to_all | solution.py:238
  7.0 0.7 reshape.51
  7.8 0.7 dynamic-slice_reduce_fusion.rows_ref
  8.5 6.7 %take_rows.1 = f32[32,4,8,128]{3,2,1,0:T(8,128)} custom-call(s32[32]{0:T(128)} %dynamic-slice_reduce_fusion.rows_ref, s32[1]{0:T(128)} %bitcast.1.half_ref, f32[8,128,1024]{2,1,0:T(8,128)} %slab_ref.1), custom_call_target="tpu_custom_call" | custom-call | tf_op jit(solution)/shard_map/take_rows/pallas_call | solution.py:41
  15.2 0.0 all-to-all-done
  15.2 11.6 %all-to-all-start.1 = ((f32[32,4,8,128]{3,2,1,0:T(8,128)}), f32[32,4,8,128]{3,2,1,0:T(8,128)S(1)}, u32[]{:S(2)}, u32[]{:S(2)}) async-start(f32[32,4,8,128]{3,2,1,0:T(8,128)} %take_rows.1), calls=%async_computation.1 | async-start | bytes 1048576 | tf_op jit(solution)/shard_map/all_to_all | solution.py:238
  26.8 0.5 broadcast.9
  27.3 0.7 reduce.5
  28.0 0.6 reshape.49.angles_ref
  28.6 15.9 %all-to-all-done.1 = f32[32,4,8,128]{3,2,1,0:T(8,128)S(1)} async-done(((f32[32,4,8,128]{3,2,1,0:T(8,128)}), f32[32,4,8,128]{3,2,1,0:T(8,128)S(1)}, u32[]{:S(2)}, u32[]{:S(2)}) %all-to-all-start.1) | async-done | bytes 524320 | tf_op jit(solution)/shard_map/all_to_all | solution.py:238
  44.5 0.0 copy-start
  44.5 0.8 copy-done
  45.3 64.6 %project.1 = f32[32,8,128]{2,1,0:T(8,128)} custom-call(s32[32]{0:T(128)} %reshape.49.angles_ref, s32[1]{0:T(128)} %bitcast.first_ref, f32[128,8,128]{2,1,0:T(8,128)} %bitcast.21), custom_call_target="tpu_custom_call" | custom-call | tf_op jit(solution)/shard_map/project/pallas_call | solution.py:142
  109.9 5.7 %all-to-all-start.2 = ((f32[8,4,8,128]{3,2,1,0:T(8,128)}), f32[8,4,8,128]{3,2,1,0:T(8,128)S(1)}, u32[]{:S(2)}, u32[]{:S(2)}) async-start(f32[8,4,8,128]{3,2,1,0:T(8,128)} %bitcast.25), calls=%async_computation.2 | async-start | bytes 262144 | tf_op jit(solution)/shard_map/all_to_all | solution.py:238
  115.6 0.0 copy-done.2
  115.7 6.7 %all-to-all-done.2 = f32[8,4,8,128]{3,2,1,0:T(8,128)S(1)} async-done(((f32[8,4,8,128]{3,2,1,0:T(8,128)}), f32[8,4,8,128]{3,2,1,0:T(8,128)S(1)}, u32[]{:S(2)}, u32[]{:S(2)}) %all-to-all-start.2) | async-done | bytes 131104 | tf_op jit(solution)/shard_map/all_to_all | solution.py:238
  122.3 0.9 broadcast_in_dim.7
  123.2 3.5 %all-to-all-start.3 = ((f32[8,4,4,8,128]{4,3,2,1,0:T(8,128)}), f32[8,4,4,8,128]{4,3,2,1,0:T(8,128)S(1)}, u32[]{:S(2)}, u32[]{:S(2)}) async-start(f32[8,4,4,8,128]{4,3,2,1,0:T(8,128)} %broadcast_in_dim.7), calls=%async_computation.3 | async-start | bytes 1048576 | tf_op jit(solution)/shard_map/all_to_all | solution.py:238
  126.7 8.6 %all-to-all-done.3 = f32[8,4,4,8,128]{4,3,2,1,0:T(8,128)S(1)} async-done(((f32[8,4,4,8,128]{4,3,2,1,0:T(8,128)}), f32[8,4,4,8,128]{4,3,2,1,0:T(8,128)S(1)}, u32[]{:S(2)}, u32[]{:S(2)}) %all-to-all-start.3) | async-done | bytes 524320 | tf_op jit(solution)/shard_map/all_to_all | solution.py:238
  135.3 0.0 copy-start.1
  135.3 0.8 copy-done.1
  136.1 30.3 %backproject.1 = f32[32,4,8,128]{3,2,1,0:T(8,128)} custom-call(s32[32]{0:T(128)} %reshape.49.angles_ref, s32[1]{0:T(128)} %bitcast.7.first_ref, f32[128,8,128]{2,1,0:T(8,128)} %bitcast.22), custom_call_target="tpu_custom_call" | custom-call | tf_op jit(solution)/shard_map/backproject/pallas_call | solution.py:203
  166.5 22.9 %all_to_all.31 = f32[32,4,8,128]{3,2,1,0:T(8,128)} all-to-all(f32[32,4,8,128]{3,2,1,0:T(8,128)} %backproject.1), channel_id=1, replica_groups=mesh['gz'=32,'vert'=8] {'gz'}, dimensions={0} | all-to-all | bytes 1048576 | tf_op jit(solution)/shard_map/all_to_all | solution.py:238
  189.3 2.1 %place.1 = f32[128,8,128]{2,1,0:T(8,128)} custom-call(s32[128]{0:T(128)} %rows_ref.1, f32[128,8,128]{2,1,0:T(8,128)} %bitcast.24), custom_call_target="tpu_custom_call" | custom-call | tf_op jit(solution)/shard_map/place/pallas_call | solution.py:228
  191.4 3.5 %all-to-all-start.5 = ((f32[8,16,8,128]{3,2,1,0:T(8,128)}), f32[8,16,8,128]{3,2,1,0:T(8,128)S(1)}, u32[]{:S(2)}, u32[]{:S(2)}) async-start(f32[8,16,8,128]{3,2,1,0:T(8,128)} %bitcast.23), calls=%async_computation.5 | async-start | bytes 1048576 | tf_op jit(solution)/shard_map/all_to_all | solution.py:238
  194.9 0.7 reshape.57
  195.5 9.0 %all-to-all-done.5 = f32[8,16,8,128]{3,2,1,0:T(8,128)S(1)} async-done(((f32[8,16,8,128]{3,2,1,0:T(8,128)}), f32[8,16,8,128]{3,2,1,0:T(8,128)S(1)}, u32[]{:S(2)}, u32[]{:S(2)}) %all-to-all-start.5) | async-done | bytes 524320 | tf_op jit(solution)/shard_map/all_to_all | solution.py:238
  204.6 0.9 reshape.61
  (3 shorter events, 0.1 us)
Async XLA Ops:
  0.6 115.0 %copy-start.2 = (f32[4,4,1024]{2,1,0:T(4,128)S(1)}, f32[4,4,1024]{2,1,0:T(4,128)}, u32[]{:S(2)}) copy-start(f32[4,4,1024]{2,1,0:T(4,128)} %param.7) | copy-start | bytes 196612
  1.9 13.3 %all-to-all-start = ((s32[8,1,4]{2,1,0:T(1,128)}), s32[8,1,4]{2,1,0:T(1,128)S(1)}, u32[]{:S(2)}, u32[]{:S(2)}) async-start(s32[8,1,4]{2,1,0:T(1,128)} %broadcast_in_dim.6), calls=%async_computation | async-start | bytes 8192 | tf_op jit(solution)/shard_map/all_to_all | solution.py:238
  15.2 29.3 %all-to-all-start.1 = ((f32[32,4,8,128]{3,2,1,0:T(8,128)}), f32[32,4,8,128]{3,2,1,0:T(8,128)S(1)}, u32[]{:S(2)}, u32[]{:S(2)}) async-start(f32[32,4,8,128]{3,2,1,0:T(8,128)} %take_rows.1), calls=%async_computation.1 | async-start | bytes 1048576 | tf_op jit(solution)/shard_map/all_to_all | solution.py:238
  44.5 0.8 copy-start
  109.9 12.4 %all-to-all-start.2 = ((f32[8,4,8,128]{3,2,1,0:T(8,128)}), f32[8,4,8,128]{3,2,1,0:T(8,128)S(1)}, u32[]{:S(2)}, u32[]{:S(2)}) async-start(f32[8,4,8,128]{3,2,1,0:T(8,128)} %bitcast.25), calls=%async_computation.2 | async-start | bytes 262144 | tf_op jit(solution)/shard_map/all_to_all | solution.py:238
  123.2 12.1 %all-to-all-start.3 = ((f32[8,4,4,8,128]{4,3,2,1,0:T(8,128)}), f32[8,4,4,8,128]{4,3,2,1,0:T(8,128)S(1)}, u32[]{:S(2)}, u32[]{:S(2)}) async-start(f32[8,4,4,8,128]{4,3,2,1,0:T(8,128)} %broadcast_in_dim.7), calls=%async_computation.3 | async-start | bytes 1048576 | tf_op jit(solution)/shard_map/all_to_all | solution.py:238
  135.3 0.8 copy-start.1
  191.4 13.2 %all-to-all-start.5 = ((f32[8,16,8,128]{3,2,1,0:T(8,128)}), f32[8,16,8,128]{3,2,1,0:T(8,128)S(1)}, u32[]{:S(2)}, u32[]{:S(2)}) async-start(f32[8,16,8,128]{3,2,1,0:T(8,128)} %bitcast.23), calls=%async_computation.5 | async-start | bytes 1048576 | tf_op jit(solution)/shard_map/all_to_all | solution.py:238

commit v2 on v1

v2 whole, which is shorter than its diff:
```python
import functools

import jax
import jax.numpy as jnp
from jax import lax
from jax.experimental import pallas as pl
from jax.experimental.pallas import tpu as pltpu
from jax.sharding import PartitionSpec as P

ANGLES = 512
LANES = 128
VMEM = pltpu.VMEM
SMEM = pltpu.SMEM
LIMIT = 24 * 1024 * 1024
VIEWS_AT_ONCE = 2
SLABS_AT_ONCE = 2


def take_rows_kernel(rows_ref, layer_ref, slab_ref, out_ref):
    count, chunks, _ = out_ref.shape
    place = lax.broadcasted_iota(jnp.int32, (chunks, LANES), 0)

    def one(item, carry):
        row = rows_ref[item]
        start = pl.multiple_of(row // 8 * 8, 8)
        inside = row - start
        found = None
        for chunk in range(chunks):
            tile = slab_ref[0, pl.ds(start, 8), pl.ds(chunk * LANES, LANES)]
            turned = pltpu.roll(tile, (chunk + 8 - inside) % 8, 0)
            found = turned if found is None else jnp.where(place == chunk, turned, found)
        out_ref[item] = found
        return carry

    lax.fori_loop(0, count, one, 0, unroll=16)


def take_rows(volume, rows, layer):
    _, row_count, columns = volume.shape
    chunks = columns // LANES
    return pl.pallas_call(
        take_rows_kernel,
        grid_spec=pltpu.PrefetchScalarGridSpec(
            num_scalar_prefetch=2,
            grid=(1,),
            in_specs=[
                pl.BlockSpec(
                    (1, row_count, columns), lambda step, rows_ref, layer_ref: (layer_ref[0], 0, 0)
                )
            ],
            out_specs=pl.BlockSpec(
                (row_count, chunks, LANES), lambda step, rows_ref, layer_ref: (0, 0, 0)
            ),
        ),
        out_shape=jax.ShapeDtypeStruct((row_count, chunks, LANES), jnp.float32),
        name="take_rows",
    )(rows, layer, volume)


def fill_padded(value, index, base_ref, diff_ref, ahead):
    zero = jnp.zeros((8, LANES), jnp.float32)
    base_ref[index, pl.ds(0, 8), :] = zero
    base_ref[index, pl.ds(8, 8), :] = zero
    base_ref[index, pl.ds(1, 8), :] = value
    padded = base_ref[index]
    rows = padded.shape[0]
    lane = lax.broadcasted_iota(jnp.int32, (rows, LANES), 1)
    if ahead:
        turned = pltpu.roll(padded, LANES - 1, 1)
        carried = pltpu.roll(turned, rows - 1, 0)
        near = jnp.where(lane == LANES - 1, carried, turned)
    else:
        turned = pltpu.roll(padded, 1, 1)
        carried = pltpu.roll(turned, 1, 0)
        near = jnp.where(lane == 0, carried, turned)
    diff_ref[index] = (near - padded) * (1.0 / ANGLES)


def shifted(base_ref, diff_ref, height, index, offset, part, lane):
    first = 1 + lax.shift_right_arithmetic(offset, 7)
    count = lax.bitwise_and(offset, LANES - 1)
    turn = lax.bitwise_and(LANES - count, LANES - 1)
    keep = lane >= count
    fraction = part.astype(jnp.float32)
    found = []
    for row in range(height):
        slot = index * height + row
        value = jnp.where(
            keep, base_ref[slot, pl.ds(first, 8), :], base_ref[slot, pl.ds(first + 1, 8), :]
        )
        diff = jnp.where(
            keep, diff_ref[slot, pl.ds(first, 8), :], diff_ref[slot, pl.ds(first + 1, 8), :]
        )
        found.append(pltpu.roll(value + fraction * diff, turn, 1))
    return found


def weight_of(slope):
    ratio = jnp.full((8, LANES), slope, jnp.int32).astype(jnp.float32) / ANGLES
    return jnp.sqrt(1.0 + ratio * ratio)


def project_kernel(angles_ref, first_ref, planes_ref, out_ref, base_ref, diff_ref):
    views, height = out_ref.shape[0], out_ref.shape[1]
    slabs = planes_ref.shape[0]
    lane = lax.broadcasted_iota(jnp.int32, (8, LANES), 1)

    def fill(slab, carry):
        for row in range(height):
            fill_padded(planes_ref[slab, row], slab * height + row, base_ref, diff_ref, True)
        return carry

    lax.fori_loop(0, slabs, fill, 0, unroll=4)

    def some_views(step, carry):
        for item in range(VIEWS_AT_ONCE):
            view = step * VIEWS_AT_ONCE + item
            slope = 2 * angles_ref[view] - ANGLES
            sums = [None] * height
            for slab in range(slabs):
                product = (first_ref[0] + 8 * slab) * slope
                moved = shifted(
                    base_ref,
                    diff_ref,
                    height,
                    slab,
                    lax.shift_right_arithmetic(product, 9),
                    lax.bitwise_and(product, ANGLES - 1),
                    lane,
                )
                sums = moved if slab == 0 else [a + b for a, b in zip(sums, moved)]
            weight = weight_of(slope)
            for row in range(height):
                out_ref[view, row] = weight * sums[row]
        return carry

    lax.fori_loop(0, views // VIEWS_AT_ONCE, some_views, 0)


def padded_call(kernel, shape, name, angles, first, rows):
    items, height, chunks, _ = rows.shape
    return pl.pallas_call(
        kernel,
        in_specs=[
            pl.BlockSpec(memory_space=SMEM),
            pl.BlockSpec(memory_space=SMEM),
            pl.BlockSpec(memory_space=VMEM),
        ],
        out_specs=pl.BlockSpec(memory_space=VMEM),
        out_shape=jax.ShapeDtypeStruct(shape, jnp.float32),
        scratch_shapes=[VMEM((items * height, 16, LANES), jnp.float32)] * 2,
        compiler_params=pltpu.CompilerParams(vmem_limit_bytes=LIMIT),
        name=name,
    )(angles, first, rows)


def backproject_kernel(
    scale, angles_ref, first_ref, rows_ref, out_ref, base_ref, diff_ref
):
    slabs, height = out_ref.shape[0], out_ref.shape[1]
    views = angles_ref.shape[0]
    lane = lax.broadcasted_iota(jnp.int32, (8, LANES), 1)

    def fill(view, carry):
        weight = weight_of(2 * angles_ref[view] - ANGLES) * scale
        for row in range(height):
            fill_padded(
                rows_ref[view, row] * weight, view * height + row, base_ref, diff_ref, False
            )
        return carry

    lax.fori_loop(0, views, fill, 0, unroll=4)

    def some_slabs(step, carry):
        for item in range(SLABS_AT_ONCE):
            slab = step * SLABS_AT_ONCE + item
            depth = first_ref[0] + 8 * slab
            sums = [None] * height
            for view in range(views):
                product = depth * (2 * angles_ref[view] - ANGLES)
                moved = shifted(
                    base_ref,
                    diff_ref,
                    height,
                    view,
                    -lax.shift_right_arithmetic(product, 9),
                    lax.bitwise_and(product, ANGLES - 1),
                    lane,
                )
                sums = moved if view == 0 else [a + b for a, b in zip(sums, moved)]
            for row in range(height):
                out_ref[slab, row] = sums[row]
        return carry

    lax.fori_loop(0, slabs // SLABS_AT_ONCE, some_slabs, 0)


def place_kernel(rows_ref, value_ref, out_ref):
    count = value_ref.shape[0]

    def one(row, carry):
        out_ref[rows_ref[row]] = value_ref[row]
        return carry

    lax.fori_loop(0, count, one, 0, unroll=8)


def place(value, rows):
    return pl.pallas_call(
        place_kernel,
        in_specs=[pl.BlockSpec(memory_space=SMEM), pl.BlockSpec(memory_space=VMEM)],
        out_specs=pl.BlockSpec(memory_space=VMEM),
        out_shape=jax.ShapeDtypeStruct(value.shape, jnp.float32),
        compiler_params=pltpu.CompilerParams(vmem_limit_bytes=LIMIT),
        name="place",
    )(rows, value)


def swap(value, axis):
    return lax.all_to_all(value, axis, 0, 0, tiled=True)


def to_all(value, axis):
    return swap(jnp.broadcast_to(value, (lax.axis_size(axis), *value.shape)), axis)


def per_device(volume, angle_index, detector_rows, measured):
    layers, row_count, columns = volume.shape
    slabs = lax.axis_size("gz")
    groups = lax.axis_size("vert")
    own_views, height, _ = measured.shape
    chunks = columns // LANES
    depth = layers * slabs
    views = own_views * groups
    vert = lax.axis_index("vert")
    first = (vert - depth // 2).reshape(1)
    angles = to_all(angle_index, "vert").reshape(views)

    sent = take_rows(volume, detector_rows, vert.reshape(1))
    planes = swap(sent.reshape(slabs, height, chunks, LANES), "gz")
    partial = padded_call(
        project_kernel, (views, height, chunks, LANES), "project", angles, first, planes
    )
    parts = swap(partial.reshape(groups, own_views, height, chunks, LANES), "vert")
    summed = jnp.sum(parts, axis=0)
    rays = measured.reshape(own_views, height, chunks, LANES)
    own = (summed - rays) * depth ** (-0.5)
    residual = own.reshape(own_views, height, columns)

    full = to_all(own, "vert").reshape(views, height, chunks, LANES)
    contrib = padded_call(
        functools.partial(backproject_kernel, views ** (-0.5)),
        (slabs, height, chunks, LANES),
        "backproject",
        angles,
        first,
        full,
    )
    layer = swap(contrib, "gz").reshape(row_count, chunks, LANES)
    ordered = place(layer, detector_rows)
    block = swap(ordered.reshape(groups, row_count // groups, chunks, LANES), "vert")
    gradient = block.reshape(layers, row_count // groups, columns)
    return (residual, gradient)


def solution(mesh):
    in_specs = (P("gz", None, None), P("vert"), P(), P("vert", "gz", None))
    out_specs = (P("vert", "gz", None), P("gz", "vert", None))
    return jax.shard_map(
        per_device, mesh=mesh, in_specs=in_specs, out_specs=out_specs, check_vma=False
    )
```

time: 206 us -> 125 us (0.61)
  Pallas kernels: 104 us -> 23.6 us
  blocking collectives: 22.9 us -> 35.5 us
  waiting for transfers between devices: 40.2 us -> 34.8 us
  local copies, waits for them, and re-layouts: 7.89 us -> 2.86 us
  starting transfers between devices: 29.4 us -> 26 us
    pallas_call x2, Pallas kernels: 95 us -> 15.5 us  [padded_call(): pl.pallas_call(kernel, in_specs=[pl.BlockSpec(memory_space=SMEM), pl.Bloc...]
    all_to_all x1 -> x2, blocking collectives: 22.9 us -> 35.5 us  [swap(): return lax.all_to_all(value, axis, 0, 0, tiled=True)]
    all_to_all x5 -> x4, waiting for transfers between devices: 40.2 us -> 34.8 us  [swap(): return lax.all_to_all(value, axis, 0, 0, tiled=True)]
    all_to_all x5 -> x4, starting transfers between devices: 29.4 us -> 26 us  [swap(): return lax.all_to_all(value, axis, 0, 0, tiled=True)]
  transfers between devices with their start and end apart: 5 -> 4, of which waited for: 4 -> 3; matrix products, arithmetic and copies ran while one was open for 2% -> 2% of each run, Pallas kernels for 3% -> 5%
where the time goes in v2:
time: 125 us
  blocking collectives  35.5 us (28%)
  waiting for transfers between devices  34.8 us (28%)
  starting transfers between devices  26 us (21%)
  Pallas kernels  23.6 us (19%)
  local copies, waits for them, and re-layouts  2.86 us (2%)
  other arithmetic  1.36 us (1%)
    all_to_all x2, blocking collectives, swap(): return lax.all_to_all(value, axis, 0, 0, tiled=True)  35.5 us
    all_to_all x4, waiting for transfers between devices, swap(): return lax.all_to_all(value, axis, 0, 0, tiled=True)  34.8 us
    all_to_all x4, starting transfers between devices, swap(): return lax.all_to_all(value, axis, 0, 0, tiled=True)  26 us
    pallas_call x2, Pallas kernels, padded_call(): pl.pallas_call(kernel, in_specs=[pl.BlockSpec(memory_space=SMEM), pl.Bloc...  15.5 us
    pallas_call x1, Pallas kernels, take_rows(): pl.pallas_call(take_rows_kernel, grid_spec=pltpu.PrefetchScalarGridSpec(n...  6.55 us
  transfers between devices with their start and end apart: 4, of which 3 were waited for; matrix products, arithmetic and copies ran while one was open for 2% of the time, Pallas kernels for 5%

profile of v2, /device:TPU:4, one launch (start us, length us, event | category | flops | bytes accessed | tf_op | source)
XLA Modules:
  0.0 124.8 jit_solution(6743517572151771543)
XLA Ops:
  0.6 0.0 copy-start.1
  0.6 1.3 %broadcast_in_dim.6 = s32[8,1,4]{2,1,0:T(1,128)} broadcast(s32[4]{0:T(128)} %param.5), dimensions={2} | broadcast | bytes 144 | tf_op jit(solution)/shard_map/broadcast_in_dim | solution.py:224
  1.9 5.1 %all-to-all-start = ((s32[8,1,4]{2,1,0:T(1,128)}), s32[8,1,4]{2,1,0:T(1,128)S(1)}, u32[]{:S(2)}, u32[]{:S(2)}) async-start(s32[8,1,4]{2,1,0:T(1,128)} %broadcast_in_dim.6), calls=%async_computation | async-start | bytes 8192 | tf_op jit(solution)/shard_map/all_to_all | solution.py:220
  7.0 6.5 %take_rows.1 = f32[128,8,128]{2,1,0:T(8,128)} custom-call(s32[128]{0:T(128)} %rows_ref.3, s32[1]{0:T(128)} %bitcast.1.layer_ref, f32[8,128,1024]{2,1,0:T(8,128)} %slab_ref.1), custom_call_target="tpu_custom_call" | custom-call | tf_op jit(solution)/shard_map/take_rows/pallas_call | solution.py:41
  13.6 0.0 copy-start
  13.6 0.0 all-to-all-done
  13.6 11.7 %all-to-all-start.1 = ((f32[32,4,8,128]{3,2,1,0:T(8,128)}), f32[32,4,8,128]{3,2,1,0:T(8,128)S(1)}, u32[]{:S(2)}, u32[]{:S(2)}) async-start(f32[32,4,8,128]{3,2,1,0:T(8,128)} %bitcast.13), calls=%async_computation.1 | async-start | bytes 1048576 | tf_op jit(solution)/shard_map/all_to_all | solution.py:220
  25.3 0.5 broadcast.7
  25.8 0.7 reduce.3
  26.5 0.1 reshape.41.angles_ref
  26.6 16.4 %all-to-all-done.1.planes_ref = f32[32,4,8,128]{3,2,1,0:T(8,128)S(1)} async-done(((f32[32,4,8,128]{3,2,1,0:T(8,128)}), f32[32,4,8,128]{3,2,1,0:T(8,128)S(1)}, u32[]{:S(2)}, u32[]{:S(2)}) %all-to-all-start.1) | async-done | bytes 524320 | tf_op jit(solution)/shard_map/all_to_all | solution.py:220
  43.0 8.1 %project.1 = f32[32,4,8,128]{3,2,1,0:T(8,128)} custom-call(s32[32]{0:T(128)S(1)} %reshape.41.angles_ref, s32[1]{0:T(128)} %bitcast.first_ref, f32[32,4,8,128]{3,2,1,0:T(8,128)S(1)} %all-to-all-done.1.planes_ref), custom_call_target="tpu_custom_call" | custom-call | tf_op jit(solution)/shard_map/project/pallas_call | solution.py:142
  51.1 5.7 %all-to-all-start.2 = ((f32[8,4,4,8,128]{4,3,2,1,0:T(8,128)}), f32[8,4,4,8,128]{4,3,2,1,0:T(8,128)S(1)}, u32[]{:S(2)}, u32[]{:S(2)}) async-start(f32[8,4,4,8,128]{4,3,2,1,0:T(8,128)} %bitcast.3), calls=%async_computation.2 | async-start | bytes 1048576 | tf_op jit(solution)/shard_map/all_to_all | solution.py:220
  56.8 0.0 copy-done.1
  56.8 9.4 %all-to-all-done.2 = f32[8,4,4,8,128]{4,3,2,1,0:T(8,128)S(1)} async-done(((f32[8,4,4,8,128]{4,3,2,1,0:T(8,128)}), f32[8,4,4,8,128]{4,3,2,1,0:T(8,128)S(1)}, u32[]{:S(2)}, u32[]{:S(2)}) %all-to-all-start.2) | async-done | bytes 524320 | tf_op jit(solution)/shard_map/all_to_all | solution.py:220
  66.3 0.1 broadcast_in_dim.7
  66.4 11.4 %all_to_all.31 = f32[8,4,4,8,128]{4,3,2,1,0:T(8,128)S(1)} all-to-all(f32[8,4,4,8,128]{4,3,2,1,0:T(8,128)S(1)} %broadcast_in_dim.7), channel_id=1, replica_groups=mesh['gz'=32,'vert'=8] {'vert'}, dimensions={0} | all-to-all | bytes 1048576 | tf_op jit(solution)/shard_map/all_to_all | solution.py:220
  77.8 7.3 %backproject.1 = f32[32,4,8,128]{3,2,1,0:T(8,128)S(1)} custom-call(s32[32]{0:T(128)S(1)} %reshape.41.angles_ref, s32[1]{0:T(128)} %bitcast.first_ref, f32[32,4,8,128]{3,2,1,0:T(8,128)S(1)} %bitcast.11), custom_call_target="tpu_custom_call" | custom-call | tf_op jit(solution)/shard_map/backproject/pallas_call | solution.py:142
  85.1 24.1 %all_to_all.32 = f32[32,4,8,128]{3,2,1,0:T(8,128)S(1)} all-to-all(f32[32,4,8,128]{3,2,1,0:T(8,128)S(1)} %backproject.1), channel_id=1, replica_groups=mesh['gz'=32,'vert'=8] {'gz'}, dimensions={0} | all-to-all | bytes 1048576 | tf_op jit(solution)/shard_map/all_to_all | solution.py:220
  109.2 0.0 copy-done
  109.2 1.6 %place.1 = f32[128,8,128]{2,1,0:T(8,128)} custom-call(s32[128]{0:T(128)S(1)} %copy-done, f32[128,8,128]{2,1,0:T(8,128)S(1)} %bitcast.12), custom_call_target="tpu_custom_call" | custom-call | tf_op jit(solution)/shard_map/place/pallas_call | solution.py:209
  110.7 3.5 %all-to-all-start.5 = ((f32[8,16,8,128]{3,2,1,0:T(8,128)}), f32[8,16,8,128]{3,2,1,0:T(8,128)S(1)}, u32[]{:S(2)}, u32[]{:S(2)}) async-start(f32[8,16,8,128]{3,2,1,0:T(8,128)} %bitcast.6), calls=%async_computation.5 | async-start | bytes 1048576 | tf_op jit(solution)/shard_map/all_to_all | solution.py:220
  114.3 0.7 subtract_multiply_fusion.1
  114.9 9.0 %all-to-all-done.5 = f32[8,16,8,128]{3,2,1,0:T(8,128)S(1)} async-done(((f32[8,16,8,128]{3,2,1,0:T(8,128)}), f32[8,16,8,128]{3,2,1,0:T(8,128)S(1)}, u32[]{:S(2)}, u32[]{:S(2)}) %all-to-all-start.5) | async-done | bytes 524320 | tf_op jit(solution)/shard_map/all_to_all | solution.py:220
  123.9 0.9 reshape.50
  (4 shorter events, 0.1 us)
Async XLA Ops:
  0.6 56.2 %copy-start.1 = (f32[4,4,1024]{2,1,0:T(4,128)S(1)}, f32[4,4,1024]{2,1,0:T(4,128)}, u32[]{:S(2)}) copy-start(f32[4,4,1024]{2,1,0:T(4,128)} %param.7) | copy-start | bytes 196612
  1.9 11.7 %all-to-all-start = ((s32[8,1,4]{2,1,0:T(1,128)}), s32[8,1,4]{2,1,0:T(1,128)S(1)}, u32[]{:S(2)}, u32[]{:S(2)}) async-start(s32[8,1,4]{2,1,0:T(1,128)} %broadcast_in_dim.6), calls=%async_computation | async-start | bytes 8192 | tf_op jit(solution)/shard_map/all_to_all | solution.py:220
  13.6 95.6 %copy-start = (s32[128]{0:T(128)S(1)}, s32[128]{0:T(128)}, u32[]{:S(2)}) copy-start(s32[128]{0:T(128)} %rows_ref.3) | copy-start | bytes 1540
  13.6 29.4 %all-to-all-start.1 = ((f32[32,4,8,128]{3,2,1,0:T(8,128)}), f32[32,4,8,128]{3,2,1,0:T(8,128)S(1)}, u32[]{:S(2)}, u32[]{:S(2)}) async-start(f32[32,4,8,128]{3,2,1,0:T(8,128)} %bitcast.13), calls=%async_computation.1 | async-start | bytes 1048576 | tf_op jit(solution)/shard_map/all_to_all | solution.py:220
  51.1 15.2 %all-to-all-start.2 = ((f32[8,4,4,8,128]{4,3,2,1,0:T(8,128)}), f32[8,4,4,8,128]{4,3,2,1,0:T(8,128)S(1)}, u32[]{:S(2)}, u32[]{:S(2)}) async-start(f32[8,4,4,8,128]{4,3,2,1,0:T(8,128)} %bitcast.3), calls=%async_computation.2 | async-start | bytes 1048576 | tf_op jit(solution)/shard_map/all_to_all | solution.py:220
  110.7 13.2 %all-to-all-start.5 = ((f32[8,16,8,128]{3,2,1,0:T(8,128)}), f32[8,16,8,128]{3,2,1,0:T(8,128)S(1)}, u32[]{:S(2)}, u32[]{:S(2)}) async-start(f32[8,16,8,128]{3,2,1,0:T(8,128)} %bitcast.6), calls=%async_computation.5 | async-start | bytes 1048576 | tf_op jit(solution)/shard_map/all_to_all | solution.py:220

commit v3 on v2

--- a/solution.py
+++ b/solution.py
@@ -16,20 +16,23 @@
 SLABS_AT_ONCE = 2
 
 
-def take_rows_kernel(rows_ref, layer_ref, slab_ref, out_ref):
+def take_rows_kernel(rows_ref, layer_ref, volume_ref, out_ref, slab_ref, sems):
     count, chunks, _ = out_ref.shape
-    place = lax.broadcasted_iota(jnp.int32, (chunks, LANES), 0)
+    copies = [
+        pltpu.make_async_copy(
+            volume_ref.at[layer_ref[0], :, pl.ds(chunk * LANES, LANES)],
+            slab_ref.at[pl.ds(chunk * count, count), :],
+            sems.at[chunk],
+        )
+        for chunk in range(chunks)
+    ]
+    for copy in copies:
+        copy.start()
+    for copy in copies:
+        copy.wait()
 
     def one(item, carry):
-        row = rows_ref[item]
-        start = pl.multiple_of(row // 8 * 8, 8)
-        inside = row - start
-        found = None
-        for chunk in range(chunks):
-            tile = slab_ref[0, pl.ds(start, 8), pl.ds(chunk * LANES, LANES)]
-            turned = pltpu.roll(tile, (chunk + 8 - inside) % 8, 0)
-            found = turned if found is None else jnp.where(place == chunk, turned, found)
-        out_ref[item] = found
+        out_ref[item] = slab_ref[pl.ds(rows_ref[item], chunks, stride=count), :]
         return carry
 
     lax.fori_loop(0, count, one, 0, unroll=16)
@@ -40,19 +43,17 @@
     chunks = columns // LANES
     return pl.pallas_call(
         take_rows_kernel,
-        grid_spec=pltpu.PrefetchScalarGridSpec(
-            num_scalar_prefetch=2,
-            grid=(1,),
-            in_specs=[
-                pl.BlockSpec(
-                    (1, row_count, columns), lambda step, rows_ref, layer_ref: (layer_ref[0], 0, 0)
-                )
-            ],
-            out_specs=pl.BlockSpec(
-                (row_count, chunks, LANES), lambda step, rows_ref, layer_ref: (0, 0, 0)
-            ),
-        ),
+        in_specs=[
+            pl.BlockSpec(memory_space=SMEM),
+            pl.BlockSpec(memory_space=SMEM),
+            pl.BlockSpec(memory_space=pl.ANY),
+        ],
+        out_specs=pl.BlockSpec(memory_space=VMEM),
         out_shape=jax.ShapeDtypeStruct((row_count, chunks, LANES), jnp.float32),
+        scratch_shapes=[
+            VMEM((row_count * chunks, LANES), jnp.float32),
+            pltpu.SemaphoreType.DMA((chunks,)),
+        ],
         name="take_rows",
     )(rows, layer, volume)
 
@@ -100,7 +101,11 @@
     return jnp.sqrt(1.0 + ratio * ratio)
 
 
-def project_kernel(angles_ref, first_ref, planes_ref, out_ref, base_ref, diff_ref):
+def project_kernel(
+    own_views, total, angles_in_ref, vert_ref, planes_ref, out_ref, base_ref, diff_ref, angles_ref
+):
+    sorted_angles(vert_ref[0], own_views, angles_in_ref, angles_ref)
+    first_depth = vert_ref[0] - total // 2
     views, height = out_ref.shape[0], out_ref.shape[1]
     slabs = planes_ref.shape[0]
     lane = lax.broadcasted_iota(jnp.int32, (8, LANES), 1)
@@ -118,7 +123,7 @@
             slope = 2 * angles_ref[view] - ANGLES
             sums = [None] * height
             for slab in range(slabs):
-                product = (first_ref[0] + 8 * slab) * slope
+                product = (first_depth + 8 * slab) * slope
                 moved = shifted(
                     base_ref,
                     diff_ref,
@@ -137,7 +142,7 @@
     lax.fori_loop(0, views // VIEWS_AT_ONCE, some_views, 0)
 
 
-def padded_call(kernel, shape, name, angles, first, rows):
+def padded_call(kernel, shape, name, angles, vert, rows):
     items, height, chunks, _ = rows.shape
     return pl.pallas_call(
         kernel,
@@ -148,15 +153,27 @@
         ],
         out_specs=pl.BlockSpec(memory_space=VMEM),
         out_shape=jax.ShapeDtypeStruct(shape, jnp.float32),
-        scratch_shapes=[VMEM((items * height, 16, LANES), jnp.float32)] * 2,
+        scratch_shapes=[VMEM((items * height, 16, LANES), jnp.float32)] * 2
+        + [SMEM(angles.shape, jnp.int32)],
         compiler_params=pltpu.CompilerParams(vmem_limit_bytes=LIMIT),
         name=name,
-    )(angles, first, rows)
+    )(angles, vert, rows)
 
 
 def backproject_kernel(
-    scale, angles_ref, first_ref, rows_ref, out_ref, base_ref, diff_ref
+    scale,
+    own_views,
+    total,
+    angles_in_ref,
+    vert_ref,
+    rows_ref,
+    out_ref,
+    base_ref,
+    diff_ref,
+    angles_ref,
 ):
+    sorted_angles(vert_ref[0], own_views, angles_in_ref, angles_ref)
+    first_depth = vert_ref[0] - total // 2
     slabs, height = out_ref.shape[0], out_ref.shape[1]
     views = angles_ref.shape[0]
     lane = lax.broadcasted_iota(jnp.int32, (8, LANES), 1)
@@ -174,7 +191,7 @@
     def some_slabs(step, carry):
         for item in range(SLABS_AT_ONCE):
             slab = step * SLABS_AT_ONCE + item
-            depth = first_ref[0] + 8 * slab
+            depth = first_depth + 8 * slab
             sums = [None] * height
             for view in range(views):
                 product = depth * (2 * angles_ref[view] - ANGLES)
@@ -220,6 +237,25 @@
     return lax.all_to_all(value, axis, 0, 0, tiled=True)
 
 
+def ring(shift, flip):
+    return [(i, (i // 2 + shift) % 4 * 2 + (i % 2) ^ flip) for i in range(8)]
+
+
+def angles_of_all(own):
+    near = jnp.concatenate([own, lax.ppermute(own, "vert", ring(0, 1))])
+    row = jnp.concatenate([near, lax.ppermute(near, "vert", ring(1, 0))])
+    return jnp.concatenate([row, lax.ppermute(row, "vert", ring(2, 0))])
+
+
+def sorted_angles(vert, own_views, angles_ref, table_ref):
+    groups = angles_ref.shape[0] // own_views
+    for block in range(groups):
+        source_y = lax.rem(vert // 2 + 4 - block // 2, 4)
+        source = 2 * source_y + lax.bitwise_xor(lax.rem(vert, 2), block % 2)
+        for view in range(own_views):
+            table_ref[source * own_views + view] = angles_ref[block * own_views + view]
+
+
 def to_all(value, axis):
     return swap(jnp.broadcast_to(value, (lax.axis_size(axis), *value.shape)), axis)
 
@@ -232,32 +268,37 @@
     chunks = columns // LANES
     depth = layers * slabs
     views = own_views * groups
-    vert = lax.axis_index("vert")
-    first = (vert - depth // 2).reshape(1)
-    angles = to_all(angle_index, "vert").reshape(views)
-
-    sent = take_rows(volume, detector_rows, vert.reshape(1))
+    vert = lax.axis_index("vert").reshape(1)
+
+    sent = take_rows(volume, detector_rows, vert)
     planes = swap(sent.reshape(slabs, height, chunks, LANES), "gz")
+    angles = angles_of_all(angle_index)
+    rays = measured.reshape(own_views, height, chunks, LANES)
+    planes, rays = lax.optimization_barrier((planes, rays))
     partial = padded_call(
-        project_kernel, (views, height, chunks, LANES), "project", angles, first, planes
+        functools.partial(project_kernel, own_views, depth),
+        (views, height, chunks, LANES),
+        "project",
+        angles,
+        vert,
+        planes,
     )
     parts = swap(partial.reshape(groups, own_views, height, chunks, LANES), "vert")
-    summed = jnp.sum(parts, axis=0)
-    rays = measured.reshape(own_views, height, chunks, LANES)
-    own = (summed - rays) * depth ** (-0.5)
-    residual = own.reshape(own_views, height, columns)
+    own = (jnp.sum(parts, axis=0) - rays) * depth ** (-0.5)
 
     full = to_all(own, "vert").reshape(views, height, chunks, LANES)
     contrib = padded_call(
-        functools.partial(backproject_kernel, views ** (-0.5)),
+        functools.partial(backproject_kernel, views ** (-0.5), own_views, depth),
         (slabs, height, chunks, LANES),
         "backproject",
         angles,
-        first,
+        vert,
         full,
     )
     layer = swap(contrib, "gz").reshape(row_count, chunks, LANES)
     ordered = place(layer, detector_rows)
+    residual = own.reshape(own_views, height, columns)
+    ordered, residual = lax.optimization_barrier((ordered, residual))
     block = swap(ordered.reshape(groups, row_count // groups, chunks, LANES), "vert")
     gradient = block.reshape(layers, row_count // groups, columns)
     return (residual, gradient)

time: 125 us -> 113 us (0.904)
  waiting for transfers between devices: 34.8 us -> 29.5 us
  Pallas kernels: 23.6 us -> 19.5 us
  starting transfers between devices: 26 us -> 22.9 us
  blocking collectives: 35.5 us -> 37.7 us
    all_to_all x4 -> x2, waiting for transfers between devices: 34.8 us -> 20.9 us  [swap(): return lax.all_to_all(value, axis, 0, 0, tiled=True)]
    ppermute x0 -> x3, waiting for transfers between devices: none -> 8.63 us  [the longest x1 3.2 us: angles_of_all(): row = jnp.concatenate([near, lax.ppermute(near, 'vert', ring(1, 0))])]
    all_to_all x4 -> x2, starting transfers between devices: 26 us -> 18 us  [swap(): return lax.all_to_all(value, axis, 0, 0, tiled=True)]
    ppermute x0 -> x3, starting transfers between devices: none -> 4.88 us  [the longest x1 2.01 us: angles_of_all(): return jnp.concatenate([row, lax.ppermute(row, 'vert', ring(2, 0))])]
    pallas_call x1, Pallas kernels: 6.55 us -> 3.32 us  [take_rows(): pl.pallas_call(take_rows_kernel, in_specs=[pl.BlockSpec(memory_space=SMEM...]
    all_to_all x2 -> x3, blocking collectives: 35.5 us -> 37.7 us  [swap(): return lax.all_to_all(value, axis, 0, 0, tiled=True)]
    broadcast_in_dim x2 -> x1, local copies, waits for them, and re-layouts: 1.33 us -> 0.05 us  [to_all(): jnp.broadcast_to(value, (lax.axis_size(axis), *value.shape))]
  transfers between devices with their start and end apart: 4 -> 5, of which waited for: 3 -> 5; matrix products, arithmetic and copies ran while one was open for 2% -> 1% of each run, Pallas kernels for 5% -> 0%
where the time goes in v3:
time: 113 us; the launch traced here: 112 us
  blocking collectives  37.7 us (33%)
  waiting for transfers between devices  29.5 us (26%)
  starting transfers between devices  22.9 us (20%)
  Pallas kernels  19.5 us (17%)
  local copies, waits for them, and re-layouts  1.62 us (1%)
    all_to_all x3, blocking collectives, swap(): return lax.all_to_all(value, axis, 0, 0, tiled=True)  37.7 us
    all_to_all x2, waiting for transfers between devices, swap(): return lax.all_to_all(value, axis, 0, 0, tiled=True)  20.9 us
    all_to_all x2, starting transfers between devices, swap(): return lax.all_to_all(value, axis, 0, 0, tiled=True)  18 us
    pallas_call x2, Pallas kernels, padded_call(): pl.pallas_call(kernel, in_specs=[pl.BlockSpec(memory_space=SMEM), pl.Bloc...  15.5 us
    pallas_call x1, Pallas kernels, take_rows(): pl.pallas_call(take_rows_kernel, in_specs=[pl.BlockSpec(memory_space=SMEM...  3.32 us
    ppermute x1, waiting for transfers between devices, angles_of_all(): row = jnp.concatenate([near, lax.ppermute(near, 'vert', ring(1, 0))])  3.2 us
    ppermute x1, waiting for transfers between devices, angles_of_all(): return jnp.concatenate([row, lax.ppermute(row, 'vert', ring(2, 0))])  3.06 us
    ppermute x1, waiting for transfers between devices, angles_of_all(): near = jnp.concatenate([own, lax.ppermute(own, 'vert', ring(0, 1))])  2.37 us
  transfers between devices with their start and end apart: 5, of which 5 were waited for; matrix products, arithmetic and copies ran while one was open for 1% of the time, Pallas kernels for 0%

profile of v3, /device:TPU:4, one launch (start us, length us, event | category | flops | bytes accessed | tf_op | source)
XLA Modules:
  0.0 112.3 jit_solution(4308681291361239420)
XLA Ops:
  0.6 0.0 copy-start.2
  0.6 0.0 copy-start.1
  0.7 3.3 %take_rows.1 = f32[128,8,128]{2,1,0:T(8,128)} custom-call(s32[128]{0:T(128)} %rows_ref.3, s32[1]{0:T(128)} %bitcast.layer_ref.vert_ref, f32[8,128,1024]{2,1,0:T(8,128)} %volume_ref.1), custom_call_target="tpu_custom_call" | custom-call | tf_op jit(solution)/shard_map/take_rows/pallas_call | solution.py:44
  4.0 0.0 copy-start
  4.0 11.6 %all-to-all-start = ((f32[32,4,8,128]{3,2,1,0:T(8,128)}), f32[32,4,8,128]{3,2,1,0:T(8,128)S(1)}, u32[]{:S(2)}, u32[]{:S(2)}) async-start(f32[32,4,8,128]{3,2,1,0:T(8,128)} %bitcast.14), calls=%async_computation | async-start | bytes 1048576 | tf_op jit(solution)/shard_map/all_to_all | solution.py:237
  15.6 0.0 copy-done.2
  15.6 1.3 %collective-permute-start = (s32[4]{0:T(128)S(1)}, s32[4]{0:T(128)S(1)}, u32[]{:S(2)}, u32[]{:S(2)}) collective-permute-start(s32[4]{0:T(128)S(1)} %copy-done.2), channel_id=1, source_target_pairs={{0,1},{1,0},{2,3},{3,2},{4,5},{5,4},{6,7},{7,6},{8,9},{9,8},{10,11... | collective-permute-start | bytes 56 | tf_op jit(solution)/shard_map/ppermute | solution.py:245
  16.9 2.4 %collective-permute-done = s32[4]{0:T(128)S(1)} collective-permute-done((s32[4]{0:T(128)S(1)}, s32[4]{0:T(128)S(1)}, u32[]{:S(2)}, u32[]{:S(2)}) %collective-permute-start) | collective-permute-done | bytes 48 | tf_op jit(solution)/shard_map/ppermute | solution.py:245
  19.3 0.1 pad_add_fusion
  19.3 1.6 %collective-permute-start.1 = (s32[8]{0:T(128)S(1)}, s32[8]{0:T(128)S(1)}, u32[]{:S(2)}, u32[]{:S(2)}) collective-permute-start(s32[8]{0:T(128)S(1)} %pad_add_fusion), channel_id=1, source_target_pairs={{0,2},{1,3},{2,4},{3,5},{4,6},{5,7},{6,0},{7,1},{8,10},{9,11},{10,... | collective-permute-start | bytes 104 | tf_op jit(solution)/shard_map/ppermute | solution.py:246
  20.9 3.2 %collective-permute-done.1 = s32[8]{0:T(128)S(1)} collective-permute-done((s32[8]{0:T(128)S(1)}, s32[8]{0:T(128)S(1)}, u32[]{:S(2)}, u32[]{:S(2)}) %collective-permute-start.1) | collective-permute-done | bytes 64 | tf_op jit(solution)/shard_map/ppermute | solution.py:246
  24.1 0.1 pad_add_fusion.1
  24.2 2.0 %collective-permute-start.2 = (s32[16]{0:T(128)S(1)}, s32[16]{0:T(128)S(1)}, u32[]{:S(2)}, u32[]{:S(2)}) collective-permute-start(s32[16]{0:T(128)S(1)} %pad_add_fusion.1), channel_id=1, source_target_pairs={{0,4},{1,5},{2,6},{3,7},{4,0},{5,1},{6,2},{7,3},{8,12},{9,13},{10,... | collective-permute-start | bytes 200 | tf_op jit(solution)/shard_map/ppermute | solution.py:247
  26.2 0.0 copy-done.1
  26.2 3.1 %collective-permute-done.2 = s32[16]{0:T(128)S(1)} collective-permute-done((s32[16]{0:T(128)S(1)}, s32[16]{0:T(128)S(1)}, u32[]{:S(2)}, u32[]{:S(2)}) %collective-permute-start.2) | collective-permute-done | bytes 96 | tf_op jit(solution)/shard_map/ppermute | solution.py:247
  29.3 0.1 pad_add_fusion.2.angles_in_ref
  29.4 3.9 %all-to-all-done.planes_ref = f32[32,4,8,128]{3,2,1,0:T(8,128)S(1)} async-done(((f32[32,4,8,128]{3,2,1,0:T(8,128)}), f32[32,4,8,128]{3,2,1,0:T(8,128)S(1)}, u32[]{:S(2)}, u32[]{:S(2)}) %all-to-all-start) | async-done | bytes 524320 | tf_op jit(solution)/shard_map/all_to_all | solution.py:237
  33.3 7.3 %project.1 = f32[32,4,8,128]{3,2,1,0:T(8,128)S(1)} custom-call(s32[32]{0:T(128)S(1)} %pad_add_fusion.2.angles_in_ref, s32[1]{0:T(128)} %bitcast.layer_ref.vert_ref, f32[32,4,8,128]{3,2,1,0:T(8,128)S(1)} %all-to-all-done.planes_ref), custom_call_target="tpu_custom_call" | custom-call | tf_op jit(solution)/shard_map/project/pallas_call | solution.py:147
  40.6 14.4 %all_to_all.25 = f32[8,4,4,8,128]{4,3,2,1,0:T(8,128)S(1)} all-to-all(f32[8,4,4,8,128]{4,3,2,1,0:T(8,128)S(1)} %bitcast.11), channel_id=1, replica_groups=mesh['gz'=32,'vert'=8] {'vert'}, dimensions={0} | all-to-all | bytes 1048576 | tf_op jit(solution)/shard_map/all_to_all | solution.py:237
  55.0 0.1 broadcast_in_dim.3
  55.1 11.2 %all_to_all.26 = f32[8,4,4,8,128]{4,3,2,1,0:T(8,128)S(1)} all-to-all(f32[8,4,4,8,128]{4,3,2,1,0:T(8,128)S(1)} %broadcast_in_dim.3), channel_id=1, replica_groups=mesh['gz'=32,'vert'=8] {'vert'}, dimensions={0} | all-to-all | bytes 1048576 | tf_op jit(solution)/shard_map/all_to_all | solution.py:237
  66.3 8.1 %backproject.1 = f32[32,4,8,128]{3,2,1,0:T(8,128)} custom-call(s32[32]{0:T(128)S(1)} %pad_add_fusion.2.angles_in_ref, s32[1]{0:T(128)} %bitcast.layer_ref.vert_ref, f32[32,4,8,128]{3,2,1,0:T(8,128)S(1)} %bitcast.10), custom_call_target="tpu_custom_call" | custom-call | tf_op jit(solution)/shard_map/backproject/pallas_call | solution.py:147
  74.4 6.4 %all-to-all-start.3 = ((f32[32,4,8,128]{3,2,1,0:T(8,128)}), f32[32,4,8,128]{3,2,1,0:T(8,128)S(1)}, u32[]{:S(2)}, u32[]{:S(2)}) async-start(f32[32,4,8,128]{3,2,1,0:T(8,128)} %backproject.1), calls=%async_computation.3 | async-start | bytes 1048576 | tf_op jit(solution)/shard_map/all_to_all | solution.py:237
  80.8 0.7 reshape.37
  81.5 17.0 %all-to-all-done.3 = f32[32,4,8,128]{3,2,1,0:T(8,128)S(1)} async-done(((f32[32,4,8,128]{3,2,1,0:T(8,128)}), f32[32,4,8,128]{3,2,1,0:T(8,128)S(1)}, u32[]{:S(2)}, u32[]{:S(2)}) %all-to-all-start.3) | async-done | bytes 524320 | tf_op jit(solution)/shard_map/all_to_all | solution.py:237
  98.5 0.0 copy-done
  98.5 0.8 place.1
  99.3 12.2 %all_to_all.27 = f32[8,16,8,128]{3,2,1,0:T(8,128)S(1)} all-to-all(f32[8,16,8,128]{3,2,1,0:T(8,128)S(1)} %bitcast.13), channel_id=1, replica_groups=mesh['gz'=32,'vert'=8] {'vert'}, dimensions={0} | all-to-all | bytes 1048576 | tf_op jit(solution)/shard_map/all_to_all | solution.py:237
  111.4 0.9 reshape.39
  (3 shorter events, 0.1 us)
Async XLA Ops:
  0.6 15.0 %copy-start.2 = (s32[4]{0:T(128)S(1)}, s32[4]{0:T(128)}, u32[]{:S(2)}) copy-start(s32[4]{0:T(128)} %param.5) | copy-start | bytes 52
  0.6 25.6 %copy-start.1 = (f32[4,4,1024]{2,1,0:T(4,128)S(1)}, f32[4,4,1024]{2,1,0:T(4,128)}, u32[]{:S(2)}) copy-start(f32[4,4,1024]{2,1,0:T(4,128)} %param.7) | copy-start | bytes 196612
  4.0 94.5 %copy-start = (s32[128]{0:T(128)S(1)}, s32[128]{0:T(128)}, u32[]{:S(2)}) copy-start(s32[128]{0:T(128)} %rows_ref.3) | copy-start | bytes 1540
  4.0 29.3 %all-to-all-start = ((f32[32,4,8,128]{3,2,1,0:T(8,128)}), f32[32,4,8,128]{3,2,1,0:T(8,128)S(1)}, u32[]{:S(2)}, u32[]{:S(2)}) async-start(f32[32,4,8,128]{3,2,1,0:T(8,128)} %bitcast.14), calls=%async_computation | async-start | bytes 1048576 | tf_op jit(solution)/shard_map/all_to_all | solution.py:237
  15.6 3.7 %collective-permute-start = (s32[4]{0:T(128)S(1)}, s32[4]{0:T(128)S(1)}, u32[]{:S(2)}, u32[]{:S(2)}) collective-permute-start(s32[4]{0:T(128)S(1)} %copy-done.2), channel_id=1, source_target_pairs={{0,1},{1,0},{2,3},{3,2},{4,5},{5,4},{6,7},{7,6},{8,9},{9,8},{10,11... | collective-permute-start | bytes 56 | tf_op jit(solution)/shard_map/ppermute | solution.py:245
  19.3 4.8 %collective-permute-start.1 = (s32[8]{0:T(128)S(1)}, s32[8]{0:T(128)S(1)}, u32[]{:S(2)}, u32[]{:S(2)}) collective-permute-start(s32[8]{0:T(128)S(1)} %pad_add_fusion), channel_id=1, source_target_pairs={{0,2},{1,3},{2,4},{3,5},{4,6},{5,7},{6,0},{7,1},{8,10},{9,11},{10,... | collective-permute-start | bytes 104 | tf_op jit(solution)/shard_map/ppermute | solution.py:246
  24.2 5.1 %collective-permute-start.2 = (s32[16]{0:T(128)S(1)}, s32[16]{0:T(128)S(1)}, u32[]{:S(2)}, u32[]{:S(2)}) collective-permute-start(s32[16]{0:T(128)S(1)} %pad_add_fusion.1), channel_id=1, source_target_pairs={{0,4},{1,5},{2,6},{3,7},{4,0},{5,1},{6,2},{7,3},{8,12},{9,13},{10,... | collective-permute-start | bytes 200 | tf_op jit(solution)/shard_map/ppermute | solution.py:247
  74.4 24.1 %all-to-all-start.3 = ((f32[32,4,8,128]{3,2,1,0:T(8,128)}), f32[32,4,8,128]{3,2,1,0:T(8,128)S(1)}, u32[]{:S(2)}, u32[]{:S(2)}) async-start(f32[32,4,8,128]{3,2,1,0:T(8,128)} %backproject.1), calls=%async_computation.3 | async-start | bytes 1048576 | tf_op jit(solution)/shard_map/all_to_all | solution.py:237

commit v4 on v3

--- a/solution.py
+++ b/solution.py
@@ -12,15 +12,16 @@
 VMEM = pltpu.VMEM
 SMEM = pltpu.SMEM
 LIMIT = 24 * 1024 * 1024
-VIEWS_AT_ONCE = 2
-SLABS_AT_ONCE = 2
-
-
-def take_rows_kernel(rows_ref, layer_ref, volume_ref, out_ref, slab_ref, sems):
+VIEWS_AT_ONCE = 8
+SLABS_AT_ONCE = 8
+
+
+def take_rows_kernel(rows_ref, volume_ref, out_ref, slab_ref, sems):
     count, chunks, _ = out_ref.shape
+    layer = lax.axis_index("vert")
     copies = [
         pltpu.make_async_copy(
-            volume_ref.at[layer_ref[0], :, pl.ds(chunk * LANES, LANES)],
+            volume_ref.at[layer, :, pl.ds(chunk * LANES, LANES)],
             slab_ref.at[pl.ds(chunk * count, count), :],
             sems.at[chunk],
         )
@@ -38,13 +39,12 @@
     lax.fori_loop(0, count, one, 0, unroll=16)
 
 
-def take_rows(volume, rows, layer):
+def take_rows(volume, rows):
     _, row_count, columns = volume.shape
     chunks = columns // LANES
     return pl.pallas_call(
         take_rows_kernel,
         in_specs=[
-            pl.BlockSpec(memory_space=SMEM),
             pl.BlockSpec(memory_space=SMEM),
             pl.BlockSpec(memory_space=pl.ANY),
         ],
@@ -55,7 +55,7 @@
             pltpu.SemaphoreType.DMA((chunks,)),
         ],
         name="take_rows",
-    )(rows, layer, volume)
+    )(rows, volume)
 
 
 def fill_padded(value, index, base_ref, diff_ref, ahead):
@@ -102,10 +102,11 @@
 
 
 def project_kernel(
-    own_views, total, angles_in_ref, vert_ref, planes_ref, out_ref, base_ref, diff_ref, angles_ref
+    own_views, total, angles_in_ref, planes_ref, out_ref, base_ref, diff_ref, angles_ref
 ):
-    sorted_angles(vert_ref[0], own_views, angles_in_ref, angles_ref)
-    first_depth = vert_ref[0] - total // 2
+    vert = lax.axis_index("vert")
+    sorted_angles(vert, own_views, angles_in_ref, angles_ref)
+    first_depth = vert - total // 2
     views, height = out_ref.shape[0], out_ref.shape[1]
     slabs = planes_ref.shape[0]
     lane = lax.broadcasted_iota(jnp.int32, (8, LANES), 1)
@@ -142,22 +143,19 @@
     lax.fori_loop(0, views // VIEWS_AT_ONCE, some_views, 0)
 
 
-def padded_call(kernel, shape, name, angles, vert, rows):
+def padded_call(kernel, shapes, name, angles, rows, *more):
     items, height, chunks, _ = rows.shape
+    whole = pl.BlockSpec(memory_space=VMEM)
     return pl.pallas_call(
         kernel,
-        in_specs=[
-            pl.BlockSpec(memory_space=SMEM),
-            pl.BlockSpec(memory_space=SMEM),
-            pl.BlockSpec(memory_space=VMEM),
-        ],
-        out_specs=pl.BlockSpec(memory_space=VMEM),
-        out_shape=jax.ShapeDtypeStruct(shape, jnp.float32),
+        in_specs=[pl.BlockSpec(memory_space=SMEM)] + [whole] * (1 + len(more)),
+        out_specs=[whole] * len(shapes),
+        out_shape=[jax.ShapeDtypeStruct(shape, jnp.float32) for shape in shapes],
         scratch_shapes=[VMEM((items * height, 16, LANES), jnp.float32)] * 2
         + [SMEM(angles.shape, jnp.int32)],
         compiler_params=pltpu.CompilerParams(vmem_limit_bytes=LIMIT),
         name=name,
-    )(angles, vert, rows)
+    )(angles, rows, *more)
 
 
 def backproject_kernel(
@@ -165,15 +163,17 @@
     own_views,
     total,
     angles_in_ref,
-    vert_ref,
     rows_ref,
+    own_ref,
     out_ref,
+    residual_ref,
     base_ref,
     diff_ref,
     angles_ref,
 ):
-    sorted_angles(vert_ref[0], own_views, angles_in_ref, angles_ref)
-    first_depth = vert_ref[0] - total // 2
+    vert = lax.axis_index("vert")
+    sorted_angles(vert, own_views, angles_in_ref, angles_ref)
+    first_depth = vert - total // 2
     slabs, height = out_ref.shape[0], out_ref.shape[1]
     views = angles_ref.shape[0]
     lane = lax.broadcasted_iota(jnp.int32, (8, LANES), 1)
@@ -210,24 +210,39 @@
         return carry
 
     lax.fori_loop(0, slabs // SLABS_AT_ONCE, some_slabs, 0)
-
-
-def place_kernel(rows_ref, value_ref, out_ref):
-    count = value_ref.shape[0]
+    for view in range(own_views):
+        for chunk in range(own_ref.shape[2]):
+            residual_ref[view, :, pl.ds(chunk * LANES, LANES)] = own_ref[view, :, chunk, :]
+
+
+def place_kernel(rows_ref, value_ref, out_ref, sorted_ref):
+    count, chunks, _ = value_ref.shape
 
     def one(row, carry):
-        out_ref[rows_ref[row]] = value_ref[row]
-        return carry
-
-    lax.fori_loop(0, count, one, 0, unroll=8)
+        start = pl.multiple_of(rows_ref[row] * chunks, chunks)
+        sorted_ref[pl.ds(start, chunks), :] = value_ref[row]
+        return carry
+
+    lax.fori_loop(0, count, one, 0, unroll=16)
+
+    def eight(step, carry):
+        for chunk in range(chunks):
+            out_ref[pl.ds(pl.multiple_of(step * 8, 8), 8), pl.ds(chunk * LANES, LANES)] = (
+                sorted_ref[pl.ds(step * 8 * chunks + chunk, 8, stride=chunks), :]
+            )
+        return carry
+
+    lax.fori_loop(0, count // 8, eight, 0, unroll=4)
 
 
 def place(value, rows):
+    count, chunks, _ = value.shape
     return pl.pallas_call(
         place_kernel,
         in_specs=[pl.BlockSpec(memory_space=SMEM), pl.BlockSpec(memory_space=VMEM)],
         out_specs=pl.BlockSpec(memory_space=VMEM),
-        out_shape=jax.ShapeDtypeStruct(value.shape, jnp.float32),
+        out_shape=jax.ShapeDtypeStruct((count, chunks * LANES), jnp.float32),
+        scratch_shapes=[VMEM((count * chunks, LANES), jnp.float32)],
         compiler_params=pltpu.CompilerParams(vmem_limit_bytes=LIMIT),
         name="place",
     )(rows, value)
@@ -268,39 +283,34 @@
     chunks = columns // LANES
     depth = layers * slabs
     views = own_views * groups
-    vert = lax.axis_index("vert").reshape(1)
-
-    sent = take_rows(volume, detector_rows, vert)
+
+    sent = take_rows(volume, detector_rows)
     planes = swap(sent.reshape(slabs, height, chunks, LANES), "gz")
     angles = angles_of_all(angle_index)
     rays = measured.reshape(own_views, height, chunks, LANES)
     planes, rays = lax.optimization_barrier((planes, rays))
-    partial = padded_call(
+    (partial,) = padded_call(
         functools.partial(project_kernel, own_views, depth),
-        (views, height, chunks, LANES),
+        [(views, height, chunks, LANES)],
         "project",
         angles,
-        vert,
         planes,
     )
     parts = swap(partial.reshape(groups, own_views, height, chunks, LANES), "vert")
     own = (jnp.sum(parts, axis=0) - rays) * depth ** (-0.5)
 
     full = to_all(own, "vert").reshape(views, height, chunks, LANES)
-    contrib = padded_call(
+    contrib, residual = padded_call(
         functools.partial(backproject_kernel, views ** (-0.5), own_views, depth),
-        (slabs, height, chunks, LANES),
+        [(slabs, height, chunks, LANES), (own_views, height, columns)],
         "backproject",
         angles,
-        vert,
         full,
+        own,
     )
     layer = swap(contrib, "gz").reshape(row_count, chunks, LANES)
     ordered = place(layer, detector_rows)
-    residual = own.reshape(own_views, height, columns)
-    ordered, residual = lax.optimization_barrier((ordered, residual))
-    block = swap(ordered.reshape(groups, row_count // groups, chunks, LANES), "vert")
-    gradient = block.reshape(layers, row_count // groups, columns)
+    gradient = swap(ordered.reshape(groups, row_count // groups, columns), "vert")
     return (residual, gradient)
 
 

time: 113 us -> 111 us (0.982)
  blocking collectives: 37.7 us -> 61.6 us
  waiting for transfers between devices: 29.5 us -> 12.5 us
  starting transfers between devices: 22.9 us -> 16.5 us
  Pallas kernels: 19.5 us -> 18.1 us
    all_to_all x3 -> x4, blocking collectives: 37.7 us -> 61.6 us  [swap(): return lax.all_to_all(value, axis, 0, 0, tiled=True)]
    all_to_all x2 -> x1, waiting for transfers between devices: 20.9 us -> 3.89 us  [swap(): return lax.all_to_all(value, axis, 0, 0, tiled=True)]
    all_to_all x2 -> x1, starting transfers between devices: 18 us -> 11.6 us  [swap(): return lax.all_to_all(value, axis, 0, 0, tiled=True)]
    reshape x2 -> x0, local copies, waits for them, and re-layouts: 1.53 us -> none  [the longest x1 0.88 us: per_device(): gradient = block.reshape(layers, row_count // groups, columns)]
    pallas_call x2, Pallas kernels: 15.5 us -> 14 us  [padded_call(): pl.pallas_call(kernel, in_specs=[pl.BlockSpec(memory_space=SMEM)] + [whol...]
  transfers between devices with their start and end apart: 5 -> 4, of which waited for: 5 -> 4; matrix products, arithmetic and copies ran while one was open for 1% -> 0% of each run, Pallas kernels for 0% -> 0%
where the time goes in v4:
time: 111 us
  blocking collectives  61.6 us (55%)
  Pallas kernels  18.1 us (16%)
  starting transfers between devices  16.5 us (15%)
  waiting for transfers between devices  12.5 us (11%)
    all_to_all x4, blocking collectives, swap(): return lax.all_to_all(value, axis, 0, 0, tiled=True)  61.6 us
    pallas_call x2, Pallas kernels, padded_call(): pl.pallas_call(kernel, in_specs=[pl.BlockSpec(memory_space=SMEM)] + [whol...  14 us
    all_to_all x1, starting transfers between devices, swap(): return lax.all_to_all(value, axis, 0, 0, tiled=True)  11.6 us
    all_to_all x1, waiting for transfers between devices, swap(): return lax.all_to_all(value, axis, 0, 0, tiled=True)  3.89 us
    pallas_call x1, Pallas kernels, take_rows(): pl.pallas_call(take_rows_kernel, in_specs=[pl.BlockSpec(memory_space=SMEM...  3.32 us
    ppermute x1, waiting for transfers between devices, angles_of_all(): row = jnp.concatenate([near, lax.ppermute(near, 'vert', ring(1, 0))])  3.2 us
    ppermute x1, waiting for transfers between devices, angles_of_all(): return jnp.concatenate([row, lax.ppermute(row, 'vert', ring(2, 0))])  3.06 us
    ppermute x1, waiting for transfers between devices, angles_of_all(): near = jnp.concatenate([own, lax.ppermute(own, 'vert', ring(0, 1))])  2.37 us
  transfers between devices with their start and end apart: 4, of which 4 were waited for; matrix products, arithmetic and copies ran while one was open for 0% of the time, Pallas kernels for 0%

profile of v4, /device:TPU:4, one launch (start us, length us, event | category | flops | bytes accessed | tf_op | source)
XLA Modules:
  0.0 110.6 jit_solution(15401753300104362511)
XLA Ops:
  0.6 0.0 copy-start.2
  0.6 0.0 copy-start.1
  0.6 3.3 %take_rows.1 = f32[128,8,128]{2,1,0:T(8,128)} custom-call(s32[128]{0:T(128)} %rows_ref.3, f32[8,128,1024]{2,1,0:T(8,128)} %volume_ref.1), custom_call_target="tpu_custom_call" | custom-call | tf_op jit(solution)/shard_map/take_rows/pallas_call | solution.py:45
  4.0 0.0 copy-start
  4.0 11.6 %all-to-all-start = ((f32[32,4,8,128]{3,2,1,0:T(8,128)}), f32[32,4,8,128]{3,2,1,0:T(8,128)S(1)}, u32[]{:S(2)}, u32[]{:S(2)}) async-start(f32[32,4,8,128]{3,2,1,0:T(8,128)} %bitcast.9), calls=%async_computation | async-start | bytes 1048576 | tf_op jit(solution)/shard_map/all_to_all | solution.py:252
  15.6 0.0 copy-done.2
  15.6 1.3 %collective-permute-start = (s32[4]{0:T(128)S(1)}, s32[4]{0:T(128)S(1)}, u32[]{:S(2)}, u32[]{:S(2)}) collective-permute-start(s32[4]{0:T(128)S(1)} %copy-done.2), channel_id=1, source_target_pairs={{0,1},{1,0},{2,3},{3,2},{4,5},{5,4},{6,7},{7,6},{8,9},{9,8},{10,11... | collective-permute-start | bytes 56 | tf_op jit(solution)/shard_map/ppermute | solution.py:260
  16.9 2.4 %collective-permute-done = s32[4]{0:T(128)S(1)} collective-permute-done((s32[4]{0:T(128)S(1)}, s32[4]{0:T(128)S(1)}, u32[]{:S(2)}, u32[]{:S(2)}) %collective-permute-start) | collective-permute-done | bytes 48 | tf_op jit(solution)/shard_map/ppermute | solution.py:260
  19.3 0.1 pad_add_fusion
  19.3 1.6 %collective-permute-start.1 = (s32[8]{0:T(128)S(1)}, s32[8]{0:T(128)S(1)}, u32[]{:S(2)}, u32[]{:S(2)}) collective-permute-start(s32[8]{0:T(128)S(1)} %pad_add_fusion), channel_id=1, source_target_pairs={{0,2},{1,3},{2,4},{3,5},{4,6},{5,7},{6,0},{7,1},{8,10},{9,11},{10,... | collective-permute-start | bytes 104 | tf_op jit(solution)/shard_map/ppermute | solution.py:261
  20.9 3.2 %collective-permute-done.1 = s32[8]{0:T(128)S(1)} collective-permute-done((s32[8]{0:T(128)S(1)}, s32[8]{0:T(128)S(1)}, u32[]{:S(2)}, u32[]{:S(2)}) %collective-permute-start.1) | collective-permute-done | bytes 64 | tf_op jit(solution)/shard_map/ppermute | solution.py:261
  24.1 0.1 pad_add_fusion.1
  24.2 2.0 %collective-permute-start.2 = (s32[16]{0:T(128)S(1)}, s32[16]{0:T(128)S(1)}, u32[]{:S(2)}, u32[]{:S(2)}) collective-permute-start(s32[16]{0:T(128)S(1)} %pad_add_fusion.1), channel_id=1, source_target_pairs={{0,4},{1,5},{2,6},{3,7},{4,0},{5,1},{6,2},{7,3},{8,12},{9,13},{10,... | collective-permute-start | bytes 200 | tf_op jit(solution)/shard_map/ppermute | solution.py:262
  26.2 0.0 copy-done.1
  26.2 3.1 %collective-permute-done.2 = s32[16]{0:T(128)S(1)} collective-permute-done((s32[16]{0:T(128)S(1)}, s32[16]{0:T(128)S(1)}, u32[]{:S(2)}, u32[]{:S(2)}) %collective-permute-start.2) | collective-permute-done | bytes 96 | tf_op jit(solution)/shard_map/ppermute | solution.py:262
  29.3 0.1 pad_add_fusion.2.angles_in_ref
  29.4 3.9 %all-to-all-done.planes_ref = f32[32,4,8,128]{3,2,1,0:T(8,128)S(1)} async-done(((f32[32,4,8,128]{3,2,1,0:T(8,128)}), f32[32,4,8,128]{3,2,1,0:T(8,128)S(1)}, u32[]{:S(2)}, u32[]{:S(2)}) %all-to-all-start) | async-done | bytes 524320 | tf_op jit(solution)/shard_map/all_to_all | solution.py:252
  33.3 6.7 %project.1 = f32[32,4,8,128]{3,2,1,0:T(8,128)S(1)} custom-call(s32[32]{0:T(128)S(1)} %pad_add_fusion.2.angles_in_ref, f32[32,4,8,128]{3,2,1,0:T(8,128)S(1)} %all-to-all-done.planes_ref), custom_call_target="tpu_custom_call" | custom-call | tf_op jit(solution)/shard_map/project/pallas_call | solution.py:149
  39.9 14.4 %all_to_all.25 = f32[8,4,4,8,128]{4,3,2,1,0:T(8,128)S(1)} all-to-all(f32[8,4,4,8,128]{4,3,2,1,0:T(8,128)S(1)} %bitcast.6), channel_id=1, replica_groups=mesh['gz'=32,'vert'=8] {'vert'}, dimensions={0} | all-to-all | bytes 1048576 | tf_op jit(solution)/shard_map/all_to_all | solution.py:252
  54.3 0.1 broadcast_in_dim.3
  54.4 11.2 %all_to_all.26 = f32[8,4,4,8,128]{4,3,2,1,0:T(8,128)S(1)} all-to-all(f32[8,4,4,8,128]{4,3,2,1,0:T(8,128)S(1)} %broadcast_in_dim.3), channel_id=1, replica_groups=mesh['gz'=32,'vert'=8] {'vert'}, dimensions={0} | all-to-all | bytes 1048576 | tf_op jit(solution)/shard_map/all_to_all | solution.py:252
  65.6 7.3 %backproject.1 = (f32[32,4,8,128]{3,2,1,0:T(8,128)S(1)}, f32[4,4,1024]{2,1,0:T(4,128)}) custom-call(s32[32]{0:T(128)S(1)} %pad_add_fusion.2.angles_in_ref, f32[32,4,8,128]{3,2,1,0:T(8,128)S(1)} %bitcast.5, f32[4,4,8,128]{3,2,1,0:T(8,128)S(1)} %subtract_multiply_fusion.own_ref), custom_call_target="tpu_custom_call" | custom-call | tf_op jit(solution)/shard_map/backproject/pallas_call | solution.py:149
  73.0 23.8 %all_to_all.27 = f32[32,4,8,128]{3,2,1,0:T(8,128)S(1)} all-to-all(f32[32,4,8,128]{3,2,1,0:T(8,128)S(1)} %get-tuple-element.9), channel_id=1, replica_groups=mesh['gz'=32,'vert'=8] {'gz'}, dimensions={0} | all-to-all | bytes 1048576 | tf_op jit(solution)/shard_map/all_to_all | solution.py:252
  96.8 0.0 copy-done
  96.8 0.8 place.1
  97.6 12.2 %all_to_all.28 = f32[8,16,1024]{2,1,0:T(8,128)S(1)} all-to-all(f32[8,16,1024]{2,1,0:T(8,128)S(1)} %bitcast.8), channel_id=1, replica_groups=mesh['gz'=32,'vert'=8] {'vert'}, dimensions={0} | all-to-all | bytes 1048576 | tf_op jit(solution)/shard_map/all_to_all | solution.py:252
  109.8 0.8 copy.7
  (3 shorter events, 0.1 us)
Async XLA Ops:
  0.6 15.0 %copy-start.2 = (s32[4]{0:T(128)S(1)}, s32[4]{0:T(128)}, u32[]{:S(2)}) copy-start(s32[4]{0:T(128)} %param.5) | copy-start | bytes 52
  0.6 25.6 %copy-start.1 = (f32[4,4,1024]{2,1,0:T(4,128)S(1)}, f32[4,4,1024]{2,1,0:T(4,128)}, u32[]{:S(2)}) copy-start(f32[4,4,1024]{2,1,0:T(4,128)} %param.7) | copy-start | bytes 196612
  4.0 92.8 %copy-start = (s32[128]{0:T(128)S(1)}, s32[128]{0:T(128)}, u32[]{:S(2)}) copy-start(s32[128]{0:T(128)} %rows_ref.3) | copy-start | bytes 1540
  4.0 29.3 %all-to-all-start = ((f32[32,4,8,128]{3,2,1,0:T(8,128)}), f32[32,4,8,128]{3,2,1,0:T(8,128)S(1)}, u32[]{:S(2)}, u32[]{:S(2)}) async-start(f32[32,4,8,128]{3,2,1,0:T(8,128)} %bitcast.9), calls=%async_computation | async-start | bytes 1048576 | tf_op jit(solution)/shard_map/all_to_all | solution.py:252
  15.6 3.7 %collective-permute-start = (s32[4]{0:T(128)S(1)}, s32[4]{0:T(128)S(1)}, u32[]{:S(2)}, u32[]{:S(2)}) collective-permute-start(s32[4]{0:T(128)S(1)} %copy-done.2), channel_id=1, source_target_pairs={{0,1},{1,0},{2,3},{3,2},{4,5},{5,4},{6,7},{7,6},{8,9},{9,8},{10,11... | collective-permute-start | bytes 56 | tf_op jit(solution)/shard_map/ppermute | solution.py:260
  19.3 4.8 %collective-permute-start.1 = (s32[8]{0:T(128)S(1)}, s32[8]{0:T(128)S(1)}, u32[]{:S(2)}, u32[]{:S(2)}) collective-permute-start(s32[8]{0:T(128)S(1)} %pad_add_fusion), channel_id=1, source_target_pairs={{0,2},{1,3},{2,4},{3,5},{4,6},{5,7},{6,0},{7,1},{8,10},{9,11},{10,... | collective-permute-start | bytes 104 | tf_op jit(solution)/shard_map/ppermute | solution.py:261
  24.2 5.1 %collective-permute-start.2 = (s32[16]{0:T(128)S(1)}, s32[16]{0:T(128)S(1)}, u32[]{:S(2)}, u32[]{:S(2)}) collective-permute-start(s32[16]{0:T(128)S(1)} %pad_add_fusion.1), channel_id=1, source_target_pairs={{0,4},{1,5},{2,6},{3,7},{4,0},{5,1},{6,2},{7,3},{8,12},{9,13},{10,... | collective-permute-start | bytes 200 | tf_op jit(solution)/shard_map/ppermute | solution.py:262

commit v5 on v4

--- a/solution.py
+++ b/solution.py
@@ -12,19 +12,25 @@
 VMEM = pltpu.VMEM
 SMEM = pltpu.SMEM
 LIMIT = 24 * 1024 * 1024
-VIEWS_AT_ONCE = 8
+VIEWS_AT_ONCE = 2
 SLABS_AT_ONCE = 8
 
 
 def take_rows_kernel(rows_ref, volume_ref, out_ref, slab_ref, sems):
-    count, chunks, _ = out_ref.shape
-    layer = lax.axis_index("vert")
+    peers, tile, _ = out_ref.shape
+    _, count, columns = volume_ref.shape
+    chunks = columns // LANES
+    part = tile // chunks
+    vert = lax.axis_index("vert")
+    y, x = lax.div(vert, 2), lax.rem(vert, 2)
+    height = count // peers
     copies = [
         pltpu.make_async_copy(
-            volume_ref.at[layer, :, pl.ds(chunk * LANES, LANES)],
-            slab_ref.at[pl.ds(chunk * count, count), :],
-            sems.at[chunk],
+            volume_ref.at[x * part + layer, :, pl.ds(chunk * LANES, LANES)],
+            slab_ref.at[pl.ds((chunk * part + layer) * count, count), :],
+            sems.at[chunk * part + layer],
         )
+        for layer in range(part)
         for chunk in range(chunks)
     ]
     for copy in copies:
@@ -32,16 +38,20 @@
     for copy in copies:
         copy.wait()
 
-    def one(item, carry):
-        out_ref[item] = slab_ref[pl.ds(rows_ref[item], chunks, stride=count), :]
-        return carry
-
-    lax.fori_loop(0, count, one, 0, unroll=16)
-
-
-def take_rows(volume, rows):
-    _, row_count, columns = volume.shape
-    chunks = columns // LANES
+    def one(peer, carry):
+        row = rows_ref[height * peer + y]
+        for eight in range(tile // 8):
+            out_ref[peer, pl.ds(eight * 8, 8), :] = slab_ref[
+                pl.ds(eight * 8 * count + row, 8, stride=count), :
+            ]
+        return carry
+
+    lax.fori_loop(0, peers, one, 0, unroll=4)
+
+
+def take_rows(volume, rows, peers):
+    layers, row_count, columns = volume.shape
+    tile = layers // 2 * columns // LANES
     return pl.pallas_call(
         take_rows_kernel,
         in_specs=[
@@ -49,10 +59,10 @@
             pl.BlockSpec(memory_space=pl.ANY),
         ],
         out_specs=pl.BlockSpec(memory_space=VMEM),
-        out_shape=jax.ShapeDtypeStruct((row_count, chunks, LANES), jnp.float32),
+        out_shape=jax.ShapeDtypeStruct((peers, tile, LANES), jnp.float32),
         scratch_shapes=[
-            VMEM((row_count * chunks, LANES), jnp.float32),
-            pltpu.SemaphoreType.DMA((chunks,)),
+            VMEM((tile * row_count, LANES), jnp.float32),
+            pltpu.SemaphoreType.DMA((tile,)),
         ],
         name="take_rows",
     )(rows, volume)
@@ -102,74 +112,99 @@
 
 
 def project_kernel(
-    own_views, total, angles_in_ref, planes_ref, out_ref, base_ref, diff_ref, angles_ref
+    own_views, total, angles_in_ref, planes_ref, kept_ref, sent_ref, base_ref, diff_ref, angles_ref
 ):
     vert = lax.axis_index("vert")
+    y, x = lax.div(vert, 2), lax.rem(vert, 2)
     sorted_angles(vert, own_views, angles_in_ref, angles_ref)
-    first_depth = vert - total // 2
-    views, height = out_ref.shape[0], out_ref.shape[1]
-    slabs = planes_ref.shape[0]
+    groups, padded, _, _ = base_ref.shape
+    chunks = padded - 2
+    tile = planes_ref.shape[0] // (2 * groups)
     lane = lax.broadcasted_iota(jnp.int32, (8, LANES), 1)
-
-    def fill(slab, carry):
-        for row in range(height):
-            fill_padded(planes_ref[slab, row], slab * height + row, base_ref, diff_ref, True)
-        return carry
-
-    lax.fori_loop(0, slabs, fill, 0, unroll=4)
-
-    def some_views(step, carry):
-        for item in range(VIEWS_AT_ONCE):
-            view = step * VIEWS_AT_ONCE + item
-            slope = 2 * angles_ref[view] - ANGLES
-            sums = [None] * height
-            for slab in range(slabs):
-                product = (first_depth + 8 * slab) * slope
-                moved = shifted(
-                    base_ref,
-                    diff_ref,
-                    height,
-                    slab,
-                    lax.shift_right_arithmetic(product, 9),
-                    lax.bitwise_and(product, ANGLES - 1),
-                    lane,
+    layer = lax.broadcasted_iota(jnp.int32, (8, LANES), 0)
+    upper = layer >= 4
+    zero = jnp.zeros((8, LANES), jnp.float32)
+
+    def fill(group, carry):
+        start = group * 2 * tile
+        values = [zero]
+        for chunk in range(chunks):
+            low = planes_ref[pl.ds(start + 4 * chunk, 8), :]
+            high = planes_ref[pl.ds(start + tile + 4 * chunk - 4, 8), :]
+            values.append(jnp.where(upper, high, low))
+        values.append(zero)
+        turned = [pltpu.roll(value, LANES - 1, 1) for value in values[1:-1]] + [zero]
+        turned = [zero] + turned
+        for chunk in range(padded):
+            after = turned[min(chunk + 1, padded - 1)]
+            near = jnp.where(lane == LANES - 1, after, turned[chunk])
+            base_ref[group, chunk] = values[chunk]
+            diff_ref[group, chunk] = (near - values[chunk]) * (1.0 / ANGLES)
+        return carry
+
+    lax.fori_loop(0, groups, fill, 0, unroll=2)
+
+    depths = 8 * lax.div(layer, 4) + lax.rem(layer, 4) + 4 * x - total // 2
+
+    def one_view(view):
+        slope = 2 * angles_ref[view] - ANGLES
+        sums = [zero] * chunks
+        for group in range(groups):
+            product = (depths + 16 * group) * slope
+            offset = lax.shift_right_arithmetic(product, 9)
+            fraction = lax.bitwise_and(product, ANGLES - 1).astype(jnp.float32)
+            source = lax.shift_right_arithmetic(offset, 7) + (
+                lane < lax.bitwise_and(offset, LANES - 1)
+            ).astype(jnp.int32)
+            before, after = source < 0, source > 0
+            lanes = lax.bitwise_and(lane + offset, LANES - 1)
+            mixed = [
+                base_ref[group, chunk] + fraction * diff_ref[group, chunk]
+                for chunk in range(padded)
+            ]
+            for chunk in range(chunks):
+                value = jnp.where(
+                    before, mixed[chunk], jnp.where(after, mixed[chunk + 2], mixed[chunk + 1])
                 )
-                sums = moved if slab == 0 else [a + b for a, b in zip(sums, moved)]
-            weight = weight_of(slope)
-            for row in range(height):
-                out_ref[view, row] = weight * sums[row]
-        return carry
-
-    lax.fori_loop(0, views // VIEWS_AT_ONCE, some_views, 0)
-
-
-def padded_call(kernel, shapes, name, angles, rows, *more):
-    items, height, chunks, _ = rows.shape
+                sums[chunk] = sums[chunk] + jnp.take_along_axis(value, lanes, axis=1)
+        ratio = jnp.full((1, LANES), slope, jnp.int32).astype(jnp.float32) / ANGLES
+        weight = jnp.sqrt(1.0 + ratio * ratio)
+        return [weight * jnp.sum(value, axis=0, keepdims=True) for value in sums]
+
+    for out_ref, column in ((kept_ref, x), (sent_ref, 1 - x)):
+
+        def some_views(step, carry):
+            for item in range(VIEWS_AT_ONCE):
+                place = step * VIEWS_AT_ONCE + item
+                source_y = lax.rem(y + 4 - lax.div(place, own_views), 4)
+                view = (source_y * 2 + column) * own_views + lax.rem(place, own_views)
+                for chunk, value in enumerate(one_view(view)):
+                    out_ref[place, pl.ds(chunk, 1), :] = value
+            return carry
+
+        lax.fori_loop(0, out_ref.shape[0] // VIEWS_AT_ONCE, some_views, 0)
+
+
+def project(planes, angles, own_views, total):
+    peers, tile, _ = planes.shape
+    views = angles.shape[0]
+    chunks = tile // 4
     whole = pl.BlockSpec(memory_space=VMEM)
+    half = jax.ShapeDtypeStruct((views // 2, chunks, LANES), jnp.float32)
     return pl.pallas_call(
-        kernel,
-        in_specs=[pl.BlockSpec(memory_space=SMEM)] + [whole] * (1 + len(more)),
-        out_specs=[whole] * len(shapes),
-        out_shape=[jax.ShapeDtypeStruct(shape, jnp.float32) for shape in shapes],
-        scratch_shapes=[VMEM((items * height, 16, LANES), jnp.float32)] * 2
+        functools.partial(project_kernel, own_views, total),
+        in_specs=[pl.BlockSpec(memory_space=SMEM), whole],
+        out_specs=[whole, whole],
+        out_shape=[half, half],
+        scratch_shapes=[VMEM((peers // 2, chunks + 2, 8, LANES), jnp.float32)] * 2
         + [SMEM(angles.shape, jnp.int32)],
         compiler_params=pltpu.CompilerParams(vmem_limit_bytes=LIMIT),
-        name=name,
-    )(angles, rows, *more)
+        name="project",
+    )(angles, planes.reshape(peers * tile, LANES))
 
 
 def backproject_kernel(
-    scale,
-    own_views,
-    total,
-    angles_in_ref,
-    rows_ref,
-    own_ref,
-    out_ref,
-    residual_ref,
-    base_ref,
-    diff_ref,
-    angles_ref,
+    scale, own_views, total, angles_in_ref, rows_ref, out_ref, residual_ref, base_ref, diff_ref, angles_ref
 ):
     vert = lax.axis_index("vert")
     sorted_angles(vert, own_views, angles_in_ref, angles_ref)
@@ -178,15 +213,25 @@
     views = angles_ref.shape[0]
     lane = lax.broadcasted_iota(jnp.int32, (8, LANES), 1)
 
-    def fill(view, carry):
-        weight = weight_of(2 * angles_ref[view] - ANGLES) * scale
-        for row in range(height):
-            fill_padded(
-                rows_ref[view, row] * weight, view * height + row, base_ref, diff_ref, False
-            )
-        return carry
-
-    lax.fori_loop(0, views, fill, 0, unroll=4)
+    def sent_by(group, row, item):
+        y, x = lax.div(group, 2), lax.rem(group, 2)
+        return ((row * 2 + x) * 4 + lax.rem(row + 4 - y, 4)) * own_views + item
+
+    def fill(group, carry):
+        for item in range(own_views):
+            view = group * own_views + item
+            weight = weight_of(2 * angles_ref[view] - ANGLES) * scale
+            for row in range(height):
+                fill_padded(
+                    rows_ref[sent_by(group, row, item)] * weight,
+                    view * height + row,
+                    base_ref,
+                    diff_ref,
+                    False,
+                )
+        return carry
+
+    lax.fori_loop(0, views // own_views, fill, 0)
 
     def some_slabs(step, carry):
         for item in range(SLABS_AT_ONCE):
@@ -210,9 +255,31 @@
         return carry
 
     lax.fori_loop(0, slabs // SLABS_AT_ONCE, some_slabs, 0)
-    for view in range(own_views):
-        for chunk in range(own_ref.shape[2]):
-            residual_ref[view, :, pl.ds(chunk * LANES, LANES)] = own_ref[view, :, chunk, :]
+    for item in range(own_views):
+        for row in range(height):
+            value = rows_ref[sent_by(vert, row, item)]
+            for chunk in range(value.shape[0]):
+                residual_ref[item, pl.ds(row, 1), pl.ds(chunk * LANES, LANES)] = value[
+                    chunk : chunk + 1, :
+                ]
+
+
+def backproject(rows, angles, own_views, height, slabs, total, scale):
+    count, chunks, _ = rows.shape
+    whole = pl.BlockSpec(memory_space=VMEM)
+    return pl.pallas_call(
+        functools.partial(backproject_kernel, scale, own_views, total),
+        in_specs=[pl.BlockSpec(memory_space=SMEM), whole],
+        out_specs=[whole, whole],
+        out_shape=[
+            jax.ShapeDtypeStruct((slabs, height, chunks, LANES), jnp.float32),
+            jax.ShapeDtypeStruct((own_views, height, chunks * LANES), jnp.float32),
+        ],
+        scratch_shapes=[VMEM((count, 16, LANES), jnp.float32)] * 2
+        + [SMEM(angles.shape, jnp.int32)],
+        compiler_params=pltpu.CompilerParams(vmem_limit_bytes=LIMIT),
+        name="backproject",
+    )(angles, rows)
 
 
 def place_kernel(rows_ref, value_ref, out_ref, sorted_ref):
@@ -284,29 +351,24 @@
     depth = layers * slabs
     views = own_views * groups
 
-    sent = take_rows(volume, detector_rows)
-    planes = swap(sent.reshape(slabs, height, chunks, LANES), "gz")
+    vert = lax.axis_index("vert")
+    y = vert // 2
+    sent = take_rows(volume, detector_rows, slabs)
+    planes = swap(sent, "gz")
     angles = angles_of_all(angle_index)
-    rays = measured.reshape(own_views, height, chunks, LANES)
+    rays = jnp.take(measured, (y + jnp.arange(height)) % height, axis=1)
+    rays = jnp.swapaxes(rays, 0, 1).reshape(height, own_views, chunks, LANES)
+    rays = jnp.stack(
+        [rays[0]] + [lax.ppermute(rays[d], "vert", ring(d, 0)) for d in range(1, height)]
+    )
     planes, rays = lax.optimization_barrier((planes, rays))
-    (partial,) = padded_call(
-        functools.partial(project_kernel, own_views, depth),
-        [(views, height, chunks, LANES)],
-        "project",
-        angles,
-        planes,
-    )
-    parts = swap(partial.reshape(groups, own_views, height, chunks, LANES), "vert")
-    own = (jnp.sum(parts, axis=0) - rays) * depth ** (-0.5)
-
-    full = to_all(own, "vert").reshape(views, height, chunks, LANES)
-    contrib, residual = padded_call(
-        functools.partial(backproject_kernel, views ** (-0.5), own_views, depth),
-        [(slabs, height, chunks, LANES), (own_views, height, columns)],
-        "backproject",
-        angles,
-        full,
-        own,
+    kept, moved = project(planes, angles, own_views, depth)
+    summed = kept + lax.ppermute(moved, "vert", ring(0, 1))
+    own = (summed - rays.reshape(summed.shape)) * depth ** (-0.5)
+
+    full = to_all(own, "vert").reshape(views * height, chunks, LANES)
+    contrib, residual = backproject(
+        full, angles, own_views, height, slabs, depth, views ** (-0.5)
     )
     layer = swap(contrib, "gz").reshape(row_count, chunks, LANES)
     ordered = place(layer, detector_rows)

time: 111 us -> 107 us (0.964)
  blocking collectives: 61.6 us -> 49.1 us
  starting transfers between devices: 16.5 us -> 20.2 us
  Pallas kernels: 18.1 us -> 20.7 us
    all_to_all x4 -> x3, blocking collectives: 61.6 us -> 49.1 us  [swap(): return lax.all_to_all(value, axis, 0, 0, tiled=True)]
    ppermute x0 -> x4, waiting for transfers between devices: none -> 4.93 us  [the longest x1 3.44 us: per_device(): summed = kept + lax.ppermute(moved, 'vert', ring(0, 1))]
    ppermute x0 -> x4, starting transfers between devices: none -> 4.64 us  [the longest x3 3.72 us: per_device(): lax.ppermute(rays[d], 'vert', ring(d, 0))]
    all_to_all x1, waiting for transfers between devices: 3.89 us -> 1.41 us  [swap(): return lax.all_to_all(value, axis, 0, 0, tiled=True)]
    ppermute x1, waiting for transfers between devices: 2.37 us -> 0.01 us  [angles_of_all(): near = jnp.concatenate([own, lax.ppermute(own, 'vert', ring(0, 1))])]
    pallas_call x2, Pallas kernels: 14 us -> 15.9 us  [the longest x1 8.6 us: project(): pl.pallas_call(functools.partial(project_kernel, own_views, total), in_sp...]
  transfers between devices with their start and end apart: 4 -> 8, of which waited for: 4 -> 5; matrix products, arithmetic and copies ran while one was open for 0% -> 1% of each run, Pallas kernels for 0% -> 4%
where the time goes in v5:
time: 107 us; the launch traced here: 106 us
  blocking collectives  49.1 us (46%)
  Pallas kernels  20.7 us (19%)
  starting transfers between devices  20.2 us (19%)
  waiting for transfers between devices  13.5 us (13%)
  local copies, waits for them, and re-layouts  1.6 us (1%)
    all_to_all x3, blocking collectives, swap(): return lax.all_to_all(value, axis, 0, 0, tiled=True)  49.1 us
    all_to_all x1, starting transfers between devices, swap(): return lax.all_to_all(value, axis, 0, 0, tiled=True)  11.6 us
    pallas_call x1, Pallas kernels, project(): pl.pallas_call(functools.partial(project_kernel, own_views, total), in_sp...  8.6 us
    pallas_call x1, Pallas kernels, backproject(): pl.pallas_call(functools.partial(backproject_kernel, scale, own_views, to...  7.35 us
    pallas_call x1, Pallas kernels, take_rows(): pl.pallas_call(take_rows_kernel, in_specs=[pl.BlockSpec(memory_space=SMEM...  3.92 us
    ppermute x1, waiting for transfers between devices, angles_of_all(): row = jnp.concatenate([near, lax.ppermute(near, 'vert', ring(1, 0))])  3.81 us
    ppermute x3, starting transfers between devices, per_device(): lax.ppermute(rays[d], 'vert', ring(d, 0))  3.72 us
    ppermute x1, waiting for transfers between devices, per_device(): summed = kept + lax.ppermute(moved, 'vert', ring(0, 1))  3.44 us
  transfers between devices with their start and end apart: 8, of which 5 were waited for; matrix products, arithmetic and copies ran while one was open for 1% of the time, Pallas kernels for 4%

profile of v5, /device:TPU:4, one launch (start us, length us, event | category | flops | bytes accessed | tf_op | source)
XLA Modules:
  0.0 106.3 jit_solution(187896010473009671)
XLA Ops:
  0.6 0.0 copy-start
  0.6 0.0 copy-start.2
  0.7 1.3 %collective-permute-start = (s32[4]{0:T(128)}, s32[4]{0:T(128)S(1)}, u32[]{:S(2)}, u32[]{:S(2)}) collective-permute-start(s32[4]{0:T(128)} %param.5), channel_id=1, source_target_pairs={{0,1},{1,0},{2,3},{3,2},{4,5},{5,4},{6,7},{7,6},{8,9},{9,8},{10,11... | collective-permute-start | bytes 56 | tf_op jit(solution)/shard_map/ppermute | solution.py:327
  1.9 3.9 %take_rows.1 = f32[32,32,128]{2,1,0:T(8,128)} custom-call(s32[128]{0:T(128)} %rows_ref.3, f32[8,128,1024]{2,1,0:T(8,128)} %volume_ref.1), custom_call_target="tpu_custom_call" | custom-call | tf_op jit(solution)/shard_map/take_rows/pallas_call | solution.py:55
  5.9 0.0 copy-start.1
  5.9 11.6 %all-to-all-start = ((f32[32,32,128]{2,1,0:T(8,128)}), f32[32,32,128]{2,1,0:T(8,128)S(1)}, u32[]{:S(2)}, u32[]{:S(2)}) async-start(f32[32,32,128]{2,1,0:T(8,128)} %take_rows.1), calls=%async_computation | async-start | bytes 1048576 | tf_op jit(solution)/shard_map/all_to_all | solution.py:319
  17.5 0.0 copy-done
  17.5 0.7 gather_fusion
  18.3 0.1 broadcast_select_fusion
  18.4 3.1 %collective-permute-start.5 = (f32[4,8,128]{2,1,0:T(8,128)S(1)}, f32[4,8,128]{2,1,0:T(8,128)S(1)}, u32[]{:S(2)}, u32[]{:S(2)}) collective-permute-start(f32[4,8,128]{2,1,0:T(8,128)S(1)} %bitcast.26), channel_id=1, source_target_pairs={{0,6},{1,7},{2,0},{3,1},{4,2},{5,3},{6,4},{7,5},{8,14},{9,15},{10,... | collective-permute-start | bytes 49160 | tf_op jit(solution)/shard_map/ppermute | solution.py:362
  21.5 0.6 collective-permute-start.4
  22.1 0.0 collective-permute-done
  22.1 0.0 copy-done.2
  22.1 0.1 pad_add_fusion
  22.2 1.0 collective-permute-start.1
  23.2 3.8 %collective-permute-done.1 = s32[8]{0:T(128)S(1)} collective-permute-done((s32[8]{0:T(128)S(1)}, s32[8]{0:T(128)S(1)}, u32[]{:S(2)}, u32[]{:S(2)}) %collective-permute-start.1) | collective-permute-done | bytes 64 | tf_op jit(solution)/shard_map/ppermute | solution.py:328
  27.0 0.1 pad_add_fusion.1
  27.1 1.7 %collective-permute-start.2 = (s32[16]{0:T(128)S(1)}, s32[16]{0:T(128)S(1)}, u32[]{:S(2)}, u32[]{:S(2)}) collective-permute-start(s32[16]{0:T(128)S(1)} %pad_add_fusion.1), channel_id=1, source_target_pairs={{0,4},{1,5},{2,6},{3,7},{4,0},{5,1},{6,2},{7,3},{8,12},{9,13},{10,... | collective-permute-start | bytes 200 | tf_op jit(solution)/shard_map/ppermute | solution.py:329
  28.8 0.0 collective-permute-start.3
  28.8 3.4 %collective-permute-done.2 = s32[16]{0:T(128)S(1)} collective-permute-done((s32[16]{0:T(128)S(1)}, s32[16]{0:T(128)S(1)}, u32[]{:S(2)}, u32[]{:S(2)}) %collective-permute-start.2) | collective-permute-done | bytes 96 | tf_op jit(solution)/shard_map/ppermute | solution.py:329
  32.2 0.1 pad_add_fusion.2.angles_in_ref
  32.3 0.0 collective-permute-done.5
  32.3 0.0 collective-permute-done.4
  32.3 1.5 %collective-permute-done.3 = f32[4,8,128]{2,1,0:T(8,128)S(1)} collective-permute-done((f32[4,8,128]{2,1,0:T(8,128)S(1)}, f32[4,8,128]{2,1,0:T(8,128)S(1)}, u32[]{:S(2)}, u32[]{:S(2)}) %collective-permute-start.3) | collective-permute-done | bytes 16416 | tf_op jit(solution)/shard_map/ppermute | solution.py:362
  33.8 1.4 %all-to-all-done = f32[32,32,128]{2,1,0:T(8,128)S(1)} async-done(((f32[32,32,128]{2,1,0:T(8,128)}), f32[32,32,128]{2,1,0:T(8,128)S(1)}, u32[]{:S(2)}, u32[]{:S(2)}) %all-to-all-start) | async-done | bytes 524320 | tf_op jit(solution)/shard_map/all_to_all | solution.py:319
  35.2 8.6 %project.1 = (f32[16,8,128]{2,1,0:T(8,128)S(1)}, f32[16,8,128]{2,1,0:T(8,128)S(1)}) custom-call(s32[32]{0:T(128)S(1)} %pad_add_fusion.2.angles_in_ref, f32[1024,128]{1,0:T(8,128)S(1)} %bitcast.17), custom_call_target="tpu_custom_call" | custom-call | tf_op jit(solution)/shard_map/project/pallas_call | solution.py:194
  43.8 0.9 collective-permute-start.6
  44.7 3.4 %collective-permute-done.6 = f32[16,8,128]{2,1,0:T(8,128)S(1)} collective-permute-done((f32[16,8,128]{2,1,0:T(8,128)S(1)}, f32[16,8,128]{2,1,0:T(8,128)S(1)}, u32[]{:S(2)}, u32[]{:S(2)}) %collective-permute-start.6) | collective-permute-done | bytes 65568 | tf_op jit(solution)/shard_map/ppermute | solution.py:366
  48.2 13.2 %all_to_all.20 = f32[8,16,8,128]{3,2,1,0:T(8,128)S(1)} all-to-all(f32[8,16,8,128]{3,2,1,0:T(8,128)S(1)} %broadcast_in_dim.15), channel_id=1, replica_groups=mesh['gz'=32,'vert'=8] {'vert'}, dimensions={0} | all-to-all | bytes 1048576 | tf_op jit(solution)/shard_map/all_to_all | solution.py:319
  61.4 7.4 %backproject.1 = (f32[32,4,8,128]{3,2,1,0:T(8,128)S(1)}, f32[4,4,1024]{2,1,0:T(4,128)}) custom-call(s32[32]{0:T(128)S(1)} %pad_add_fusion.2.angles_in_ref, f32[128,8,128]{2,1,0:T(8,128)S(1)} %bitcast.18), custom_call_target="tpu_custom_call" | custom-call | tf_op jit(solution)/shard_map/backproject/pallas_call | solution.py:270
  68.7 23.7 %all_to_all.21 = f32[32,4,8,128]{3,2,1,0:T(8,128)S(1)} all-to-all(f32[32,4,8,128]{3,2,1,0:T(8,128)S(1)} %get-tuple-element.13), channel_id=1, replica_groups=mesh['gz'=32,'vert'=8] {'gz'}, dimensions={0} | all-to-all | bytes 1048576 | tf_op jit(solution)/shard_map/all_to_all | solution.py:319
  92.5 0.0 copy-done.1
  92.5 0.8 place.1
  93.3 12.2 %all_to_all.22 = f32[8,16,1024]{2,1,0:T(8,128)S(1)} all-to-all(f32[8,16,1024]{2,1,0:T(8,128)S(1)} %bitcast.20), channel_id=1, replica_groups=mesh['gz'=32,'vert'=8] {'vert'}, dimensions={0} | all-to-all | bytes 1048576 | tf_op jit(solution)/shard_map/all_to_all | solution.py:319
  105.5 0.8 copy.7
  (7 shorter events, 0.1 us)
Async XLA Ops:
  0.6 16.9 %copy-start = (f32[4,4,1024]{2,1,0:T(4,128)S(1)}, f32[4,4,1024]{2,1,0:T(4,128)}, u32[]{:S(2)}) copy-start(f32[4,4,1024]{2,1,0:T(4,128)} %param.7) | copy-start | bytes 196612
  0.6 21.5 %copy-start.2 = (s32[4]{0:T(128)S(1)}, s32[4]{0:T(128)}, u32[]{:S(2)}) copy-start(s32[4]{0:T(128)} %param.5) | copy-start | bytes 52
  0.7 21.5 %collective-permute-start = (s32[4]{0:T(128)}, s32[4]{0:T(128)S(1)}, u32[]{:S(2)}, u32[]{:S(2)}) collective-permute-start(s32[4]{0:T(128)} %param.5), channel_id=1, source_target_pairs={{0,1},{1,0},{2,3},{3,2},{4,5},{5,4},{6,7},{7,6},{8,9},{9,8},{10,11... | collective-permute-start | bytes 56 | tf_op jit(solution)/shard_map/ppermute | solution.py:327
  5.9 86.6 %copy-start.1 = (s32[128]{0:T(128)S(1)}, s32[128]{0:T(128)}, u32[]{:S(2)}) copy-start(s32[128]{0:T(128)} %rows_ref.3) | copy-start | bytes 1540
  5.9 29.3 %all-to-all-start = ((f32[32,32,128]{2,1,0:T(8,128)}), f32[32,32,128]{2,1,0:T(8,128)S(1)}, u32[]{:S(2)}, u32[]{:S(2)}) async-start(f32[32,32,128]{2,1,0:T(8,128)} %take_rows.1), calls=%async_computation | async-start | bytes 1048576 | tf_op jit(solution)/shard_map/all_to_all | solution.py:319
  18.4 13.8 %collective-permute-start.5 = (f32[4,8,128]{2,1,0:T(8,128)S(1)}, f32[4,8,128]{2,1,0:T(8,128)S(1)}, u32[]{:S(2)}, u32[]{:S(2)}) collective-permute-start(f32[4,8,128]{2,1,0:T(8,128)S(1)} %bitcast.26), channel_id=1, source_target_pairs={{0,6},{1,7},{2,0},{3,1},{4,2},{5,3},{6,4},{7,5},{8,14},{9,15},{10,... | collective-permute-start | bytes 49160 | tf_op jit(solution)/shard_map/ppermute | solution.py:362
  21.5 10.8 %collective-permute-start.4 = (f32[4,8,128]{2,1,0:T(8,128)S(1)}, f32[4,8,128]{2,1,0:T(8,128)S(1)}, u32[]{:S(2)}, u32[]{:S(2)}) collective-permute-start(f32[4,8,128]{2,1,0:T(8,128)S(1)} %bitcast.24), channel_id=1, source_target_pairs={{0,4},{1,5},{2,6},{3,7},{4,0},{5,1},{6,2},{7,3},{8,12},{9,13},{10,... | collective-permute-start | bytes 49160 | tf_op jit(solution)/shard_map/ppermute | solution.py:362
  22.2 4.8 %collective-permute-start.1 = (s32[8]{0:T(128)S(1)}, s32[8]{0:T(128)S(1)}, u32[]{:S(2)}, u32[]{:S(2)}) collective-permute-start(s32[8]{0:T(128)S(1)} %pad_add_fusion), channel_id=1, source_target_pairs={{0,2},{1,3},{2,4},{3,5},{4,6},{5,7},{6,0},{7,1},{8,10},{9,11},{10,... | collective-permute-start | bytes 104 | tf_op jit(solution)/shard_map/ppermute | solution.py:328
  27.1 5.1 %collective-permute-start.2 = (s32[16]{0:T(128)S(1)}, s32[16]{0:T(128)S(1)}, u32[]{:S(2)}, u32[]{:S(2)}) collective-permute-start(s32[16]{0:T(128)S(1)} %pad_add_fusion.1), channel_id=1, source_target_pairs={{0,4},{1,5},{2,6},{3,7},{4,0},{5,1},{6,2},{7,3},{8,12},{9,13},{10,... | collective-permute-start | bytes 200 | tf_op jit(solution)/shard_map/ppermute | solution.py:329
  28.8 4.9 %collective-permute-start.3 = (f32[4,8,128]{2,1,0:T(8,128)S(1)}, f32[4,8,128]{2,1,0:T(8,128)S(1)}, u32[]{:S(2)}, u32[]{:S(2)}) collective-permute-start(f32[4,8,128]{2,1,0:T(8,128)S(1)} %bitcast.22), channel_id=1, source_target_pairs={{0,2},{1,3},{2,4},{3,5},{4,6},{5,7},{6,0},{7,1},{8,10},{9,11},{10,... | collective-permute-start | bytes 49160 | tf_op jit(solution)/shard_map/ppermute | solution.py:362
  43.8 4.4 %collective-permute-start.6 = (f32[16,8,128]{2,1,0:T(8,128)S(1)}, f32[16,8,128]{2,1,0:T(8,128)S(1)}, u32[]{:S(2)}, u32[]{:S(2)}) collective-permute-start(f32[16,8,128]{2,1,0:T(8,128)S(1)} %get-tuple-element.10), channel_id=1, source_target_pairs={{0,1},{1,0},{2,3},{3,2},{4,5},{5,4},{6,7},{7,6},{8,9},{9,8},{10,11... | collective-permute-start | bytes 196616 | tf_op jit(solution)/shard_map/ppermute | solution.py:366
